TPU v7x, 32 devices: a whole 2x2x4 slice. The times are simulated.
32 devices in a mesh: dp: 16 (over z, y, core), tensor: 2 (over x).
Axes of the slice: x: 2, y: 2, z: 4, core: 2. Of those that a mesh axis runs over, the one named last changes fastest.
Arguments:
- attn_out: bfloat16 [12288, 2048], P('dp', 'tensor'), may hold values from -6 to 6
- out_proj_t: bfloat16 [4096, 2048], P(None, 'tensor'), may hold values from -0.09375 to 0.09375
- grad_out: bfloat16 [12288, 4096], P('dp', 'tensor'), may hold values from -6 to 6
- read_weights: float32 [12288, 16], P('dp'), may hold values from 0 to 0.0026041667
- memory_gate: float32 [256, 16], P('dp'), may hold values from -0.2 to 1
- write_pos: int32 [16, 16], P('dp'), may hold values from 0 to 767, as said below
Outputs:
- grad_attn_out: bfloat16 [12288, 2048], P('dp', 'tensor')
- grad_out_proj_t: float32 [4096, 2048], P('dp', 'tensor')
- grad_memory: float32 [256, 4096], P('dp', 'tensor')
Inputs may be any that keep to these rules, and one draw needn't show every extreme that they name: `write_pos`: the 16 positions of one segment are distinct.
All inputs are finite; a program needn't handle non-finite values.
Results may differ from a plain program's by a relative error of at most 0.0034.
Values may be sent and summed in bfloat16 or wider, within the bound.
A program may use at most 64 MiB of HBM per device.

v0:
```python
import functools

import jax
import jax.numpy as jnp
from jax import lax
from jax.experimental import pallas as pl
from jax.experimental.pallas import tpu as pltpu
from jax.sharding import PartitionSpec as P

MESH = pl.DeviceIdType.MESH
F32 = jnp.float32
BF16 = jnp.bfloat16


def split3(a):
    hi = a.astype(BF16)
    rest = a - hi.astype(F32)
    mid = rest.astype(BF16)
    low = (rest - mid.astype(F32)).astype(BF16)
    return jnp.concatenate([hi, mid, low], axis=0)


def tdot(a, b):
    return lax.dot_general(a, b, (((0,), (0,)), ((), ())), preferred_element_type=F32)


def kernel(
    n, attn_hbm, w_hbm, g_hbm, rw, gate, wpos, out_attn, out_w, out_mem,
    g, attn, w, attn_p, gx, za, zb, zp, acc, onehot, local, after, after_x,
    lsend, lrecv, asend, arecv, ysend, yrecv, kept, zsend, zrecv, mine, gpad,
    g_sem, attn_sem, w_sem, x_s, x_r, l_s, l_r, a_s, a_r, ax_s, ax_r, t_s, t_r, p_s, p_r, y_s, y_r, z_s, z_r,
):
    d = lax.axis_index("dp")
    t = lax.axis_index("tensor")
    c = lax.rem(d, 2)
    y = lax.rem(d // 2, 2)
    z = d // 4
    nz = n // 4
    seg, half = g.shape
    hd = attn.shape[1]
    slots = rw.shape[1]
    bw = 2 * half // n
    lw = half // n
    zh = nz // 2
    sub = 128
    ns = bw // sub
    nu = 2 * zh * ns
    partner = (d + 1 - 2 * c, t)
    xpeer = (d, 1 - t)
    ypeer = (d + 2 - 4 * y, t)
    tile = 256

    def remote(src, dst, ss, rs, dev):
        return pltpu.make_async_remote_copy(
            src_ref=src, dst_ref=dst, send_sem=ss, recv_sem=rs, device_id=dev, device_id_type=MESH
        )

    def peer(o):
        return lax.rem(d + o, n)

    barrier = pltpu.get_barrier_semaphore()
    for o in range(1, n):
        pl.semaphore_signal(barrier, inc=1, device_id=(peer(o), t), device_id_type=MESH)
    pl.semaphore_signal(barrier, inc=1, device_id=xpeer, device_id_type=MESH)

    gcopy = pltpu.make_async_copy(g_hbm, g, g_sem)
    gcopy.start()
    attncopy = pltpu.make_async_copy(attn_hbm, attn, attn_sem)
    attncopy.start()
    pl.semaphore_wait(barrier, n)

    def place(h, u):
        r = u // (2 * ns)
        zz = r + h * (zh - 1 - 2 * r)
        yd = 1 - y if (u // ns) % 2 == 0 else y
        return zz, 2 * zz + yd, u % ns

    def cols(h, u, par):
        _, j, piece = place(h, u)
        return pl.ds(pl.multiple_of((2 * j + par) * bw + piece * sub, sub), sub)

    xcopies = []
    for u in range(nu):
        for k in range(2):
            at = cols(t, u, 1 - c if k == 0 else c)
            i = 2 * u + k
            xcopies.append(remote(g_hbm.at[:, at], gx.at[:, at], x_s.at[i], x_r.at[i], xpeer))
    early = 5
    for copy in xcopies[:early]:
        copy.start()
    wcopy = pltpu.make_async_copy(w_hbm, w, w_sem)
    wcopy.start()
    tcopy = remote(attn_hbm, attn_p, t_s, t_r, partner)
    tcopy.start()

    three = split3(rw[...].T)
    gpad[...] = jnp.zeros_like(gpad)
    gpad[:, :slots] = gate[...].T
    gcopy.wait()
    attncopy.wait()

    def local_step(i, _):
        at = pl.ds(pl.multiple_of(i * tile, tile), tile)
        r = jnp.dot(three, g[:, at], preferred_element_type=F32)
        local[:, at] = r[:slots] + r[slots : 2 * slots] + r[2 * slots :]
        return 0

    lax.fori_loop(0, half // tile, local_step, 0)

    def msg(o):
        return local[:, pl.ds(pl.multiple_of(peer(o) * lw, lw), lw)]

    lrecv[0, :slots, :] = msg(0)
    lrecv[0, slots:, :] = gpad[...]
    lcopies = []
    for o in range(1, n):
        lsend[o, :slots, :] = msg(o)
        lsend[o, slots:, :] = gpad[...]
        lcopies.append(remote(lsend.at[o], lrecv.at[o], l_s.at[o], l_r.at[o], (peer(o), t)))
    for copy in lcopies:
        copy.start()

    place_of = lax.broadcasted_iota(jnp.int32, (seg, 3 * slots), 0)
    wide = jnp.concatenate([wpos[...]] * 3, axis=1)
    onehot[...] = jnp.where(place_of == wide, 1.0, 0.0).astype(BF16)
    for copy in lcopies:
        copy.wait_recv()

    def sweep(i, carry):
        s = n - 1 - i
        slot = lax.rem(d - s + n, n)
        target = lax.rem(s - d + n, n)
        asend[target, :slots, :] = carry
        m = lrecv[slot]
        fresh = m[:slots]
        for k in range(slots):
            fresh = fresh + m[slots:, k : k + 1] * carry[k : k + 1, :]
        asend[target, slots:, :] = fresh
        return fresh

    lax.fori_loop(0, n, sweep, jnp.zeros((slots, lw), F32))
    acopies = []
    for o in range(1, n):
        acopies.append(remote(asend.at[o], arecv.at[o], a_s.at[o], a_r.at[o], (peer(o), t)))
    for copy in acopies:
        copy.start()
    for copy in acopies:
        copy.wait_recv()
    for o in range(n):
        src = lax.rem(d - o + n, n)
        at = pl.ds(pl.multiple_of(src * lw, lw), lw)
        m = asend[0] if o == 0 else arecv[o]
        after[:, at] = m[:slots]
        out_mem[:, at] = m[slots:]
    axcopy = remote(after, after_x, ax_s, ax_r, xpeer)
    axcopy.start()
    for copy in xcopies[early:]:
        copy.start()

    def fix(src, aft, dst, at):
        written = jnp.dot(onehot[...], split3(aft[:, at]), preferred_element_type=F32)
        dst[:, at] = (src[:, at].astype(F32) + written).astype(BF16)

    pcopies = []

    def to_partner(zr, h, u, i):
        copy = remote(zr.at[:, cols(h, u, 1 - c)], zp.at[i], p_s.at[i], p_r.at[i], partner)
        copy.start()
        pcopies.append(copy)

    ncopies = []
    ycopies = {}

    def is_other(u):
        return (u // ns) % 2 == 0

    def slot_of(u, i):
        return (i // nu) * (nu // 2) + (u // (2 * ns)) * ns + u % ns

    def grad_block(zr, h, u, i, first):
        pcopies[i].wait_recv()
        if first:
            tcopy.wait_recv()
        slot = slot_of(u, i)

        def step(m, _):
            at = pl.ds(pl.multiple_of(m * tile, tile), tile)
            r = tdot(zr[:, cols(h, u, c)], attn[:, at]) + tdot(zp[i], attn_p[:, at])
            if is_other(u):
                ysend[slot, :, at] = r.astype(BF16)
            else:
                kept[slot, :, at] = r
            return 0

        lax.fori_loop(0, hd // tile, step, 0)
        if is_other(u):
            copy = remote(ysend.at[slot], yrecv.at[slot], y_s.at[slot], y_r.at[slot], ypeer)
            copy.start()
            ycopies[slot] = copy

    def to_owner(h, u, i):
        slot = slot_of(u, i)
        piece = u % ns
        zd = zh * h + place(h, u)[0]
        ycopies[slot].wait_recv()
        own = zd == z

        @pl.when(own)
        def _():
            mine[piece] = kept[slot] + yrecv[slot].astype(F32)

        @pl.when(jnp.logical_not(own))
        def _():
            o = lax.rem(zd - z + nz, nz)
            zsend[slot] = (kept[slot] + yrecv[slot].astype(F32)).astype(BF16)
            remote(
                zsend.at[slot],
                zrecv.at[o, piece],
                z_s.at[slot],
                z_r.at[o, piece],
                (zd * 4 + 2 * y + c, t),
            ).start()

        ncopies.append((own, slot))

    for u in range(nu):
        fix(g, after, za, cols(t, u, 1 - c))
        to_partner(za, t, u, u)
        fix(g, after, za, cols(t, u, c))
    for u in range(nu):
        grad_block(za, t, u, u, u == 0)
    wcopy.wait()
    for u in range(2 * ns):
        if not is_other(u):
            to_owner(t, u, u)

    def own_step(m, _):
        at = pl.ds(pl.multiple_of(m * tile, tile), tile)
        rows = pl.ds(pl.multiple_of(t * half, half), half)
        acc[:, at] = jnp.dot(za[...], w[rows, at], preferred_element_type=F32)
        return 0

    lax.fori_loop(0, hd // tile, own_step, 0)
    for u in range(2 * ns, nu):
        if not is_other(u):
            to_owner(t, u, u)

    oh = 1 - t
    axcopy.wait_recv()
    for u in range(nu):
        i = nu + u
        xcopies[2 * u].wait_recv()
        fix(gx, after_x, zb, cols(oh, u, 1 - c))
        to_partner(zb, oh, u, i)
        xcopies[2 * u + 1].wait_recv()
        fix(gx, after_x, zb, cols(oh, u, c))
        grad_block(zb, oh, u, i, False)
        if not is_other(u):
            to_owner(oh, u, i)

        if (u + 1) % ns == 0:
            wide_at = pl.multiple_of(2 * place(oh, u)[1] * bw, 2 * bw)

            def other_step(m, _, wide_at=wide_at, last=u == nu - 1):
                at = pl.ds(pl.multiple_of(m * tile, tile), tile)
                rows = pl.ds(pl.multiple_of(oh * half + wide_at, 2 * bw), 2 * bw)
                r = acc[:, at] + jnp.dot(
                    zb[:, pl.ds(wide_at, 2 * bw)], w[rows, at], preferred_element_type=F32
                )
                if last:
                    out_attn[:, at] = r.astype(BF16)
                else:
                    acc[:, at] = r
                return 0

            lax.fori_loop(0, hd // tile, other_step, 0)

    for piece in range(ns):
        total = mine[piece]
        for o in range(1, nz):
            remote(
                zrecv.at[o, piece], zrecv.at[o, piece], z_s.at[0], z_r.at[o, piece], ypeer
            ).wait_recv()
            total = total + zrecv[o, piece].astype(F32)
        out_w[pl.ds(piece * sub, sub), :] = total

    for copy in xcopies + [tcopy, axcopy] + lcopies + acopies + pcopies + list(ycopies.values()):
        copy.wait_send()
    for own, slot in ncopies:

        @pl.when(jnp.logical_not(own))
        def _():
            remote(
                zsend.at[slot], zrecv.at[0, 0], z_s.at[slot], z_r.at[0, 0], ypeer
            ).wait_send()


def fused(n, attn_out, out_proj_t, grad_out, read_weights, memory_gate, write_pos):
    seg, half = grad_out.shape
    hd = attn_out.shape[1]
    slots = write_pos.shape[1]
    depth = out_proj_t.shape[0]
    bw, lw, nz = depth // n, half // n, n // 4
    sub = 128
    ns = bw // sub
    nu = nz * ns
    V = pltpu.VMEM
    D = pltpu.SemaphoreType.DMA
    vmem = pl.BlockSpec(memory_space=pltpu.VMEM)
    return pl.pallas_call(
        functools.partial(kernel, n),
        out_shape=(
            jax.ShapeDtypeStruct((seg, hd), BF16),
            jax.ShapeDtypeStruct((bw, hd), F32),
            jax.ShapeDtypeStruct((slots, half), F32),
        ),
        in_specs=[pl.BlockSpec(memory_space=pl.ANY)] * 3 + [vmem] * 3,
        out_specs=(vmem, vmem, vmem),
        scratch_shapes=[
            V((seg, half), BF16),
            V((seg, hd), BF16),
            V((depth, hd), BF16),
            V((seg, hd), BF16),
            V((seg, half), BF16),
            V((seg, half), BF16),
            V((seg, half), BF16),
            V((2 * nu, seg, sub), BF16),
            V((seg, hd), F32),
            V((seg, 3 * slots), BF16),
            V((slots, half), F32),
            V((slots, half), F32),
            V((slots, half), F32),
            V((n, 2 * slots, lw), F32),
            V((n, 2 * slots, lw), F32),
            V((n, 2 * slots, lw), F32),
            V((n, 2 * slots, lw), F32),
            V((nu, sub, hd), BF16),
            V((nu, sub, hd), BF16),
            V((nu, sub, hd), F32),
            V((nu, sub, hd), BF16),
            V((nz, ns, sub, hd), BF16),
            V((ns, sub, hd), F32),
            V((slots, lw), F32),
            D,
            D,
            D,
            D((2 * nu,)),
            D((2 * nu,)),
            D((n,)),
            D((n,)),
            D((n,)),
            D((n,)),
            D,
            D,
            D,
            D,
            D((2 * nu,)),
            D((2 * nu,)),
            D((nu,)),
            D((nu,)),
            D((nu,)),
            D((nz, ns)),
        ],
        compiler_params=pltpu.CompilerParams(
            collective_id=0, has_side_effects=True, vmem_limit_bytes=62 * 1024 * 1024
        ),
    )(attn_out, out_proj_t, grad_out, read_weights, memory_gate, write_pos)


def plain(attn_out, out_proj_t, grad_out, read_weights, memory_gate, write_pos):
    high = lax.Precision.HIGHEST
    seg_len = attn_out.shape[0]
    slots = write_pos.shape[1]
    gate_at_step = memory_gate.T
    dy_cols = grad_out.astype(jnp.float32)
    local = jnp.dot(read_weights.T, dy_cols, precision=high, preferred_element_type=jnp.float32)
    all_gates, all_terms = (
        lax.all_gather(gate_at_step, "dp", axis=0, tiled=True),
        lax.all_gather(local, "dp", axis=0, tiled=True),
    )
    count = lax.axis_size("dp")
    mine = lax.axis_index("dp")

    def sweep(step, carry):
        which = (count - 1 - step).astype(jnp.int32)
        gate = lax.dynamic_slice_in_dim(all_gates, which * slots, slots, 0)
        term = lax.dynamic_slice_in_dim(all_terms, which * slots, slots, 0)
        fresh = jnp.dot(gate, carry, precision=high, preferred_element_type=jnp.float32) + term
        return jnp.where(which > mine, fresh, carry)

    after = lax.fori_loop(0, count, sweep, jnp.zeros_like(local))
    grad_memory = (
        jnp.dot(gate_at_step, after, precision=high, preferred_element_type=jnp.float32) + local
    )
    places = jnp.arange(seg_len, dtype=jnp.int32)
    onehot = (places[:, None] == write_pos[0][None, :]).astype(jnp.float32)
    written = jnp.dot(onehot, after, precision=high, preferred_element_type=jnp.float32)
    grad_z = (dy_cols + written).astype(jnp.bfloat16)
    full_z = lax.all_gather(grad_z, "tensor", axis=1, tiled=True)
    grad_attn = jnp.dot(full_z, out_proj_t, preferred_element_type=jnp.float32).astype(jnp.bfloat16)
    term = lax.dot_general(
        full_z, attn_out, (((0,), (0,)), ((), ())), preferred_element_type=jnp.float32
    )
    grad_weight = lax.psum_scatter(term, "dp", scatter_dimension=0, tiled=True)
    return (grad_attn, grad_weight, grad_memory)


def solution(mesh):
    n = mesh.shape["dp"]
    parts = mesh.shape["tensor"]

    def body(attn_out, out_proj_t, grad_out, read_weights, memory_gate, write_pos):
        half, hd = grad_out.shape[1], attn_out.shape[1]
        fits = (
            parts == 2
            and n % 8 == 0
            and half % (n * 128) == 0
            and half % 256 == 0
            and hd % 256 == 0
            and out_proj_t.shape[0] <= 4096
        )
        args = (attn_out, out_proj_t, grad_out, read_weights, memory_gate, write_pos)
        return fused(n, *args) if fits else plain(*args)

    return jax.shard_map(
        body,
        mesh=mesh,
        in_specs=(
            P("dp", "tensor"),
            P(None, "tensor"),
            P("dp", "tensor"),
            P("dp", None),
            P("dp", None),
            P("dp", None),
        ),
        out_specs=(P("dp", "tensor"), P("dp", "tensor"), P("dp", "tensor")),
        check_vma=False,
    )
```

profile of v0, /device:TPU:17, one launch (start us, length us, event | category | flops | bytes accessed | tf_op | source)
XLA Modules:
  0.0 118.0 jit_solution(6739034429923217847)
XLA Ops:
  0.6 1.7 %copy.9.rw = f32[768,16]{1,0:T(8,128)} copy(f32[768,16]{0,1:T(8,128)} %param.9) | data formatting | bytes 98304 | tf_op args[3]
  2.3 111.2 %shard_map.85 = (bf16[768,1024]{1,0:T(8,128)(2,1)}, f32[256,1024]{1,0:T(8,128)}, f32[16,2048]{1,0:T(8,128)}) custom-call(bf16[768,1024]{1,0:T(8,128)(2,1)} %attn_hbm.1, bf16[4096,1024]{1,0:T(8,128)(2,1)} %w_hbm.1, bf16[768,2048]{1,0:T(8,128)(2,1)} %g_hbm.1, f32[768,16]{1,0:T(8,128)} %copy.9.rw, f32[16,16]{1,0:T(8,128)} %gate.1, s32[1,16]{1,0:T(1,128)} %wpos.1), custom_call_target="tpu_custom_call" | custom-call | tf_op jit(solution)/shard_map/pallas_call | solution.py:310
  113.5 0.0 copy-start
  113.5 2.8 %copy.13 = bf16[768,1024]{1,0:T(8,128)(2,1)} copy(bf16[768,1024]{1,0:T(8,128)(2,1)} %get-tuple-element.6) | data formatting | bytes 3145728
  116.3 0.0 copy-done
  116.3 0.0 copy-start.1
  116.3 1.0 copy.14
  117.3 0.1 copy-done.1
  117.3 0.7 copy.15
Async XLA Ops:
  113.5 2.8 %copy-start = (f32[256,1024]{1,0:T(8,128)S(1)}, f32[256,1024]{1,0:T(8,128)}, u32[]{:S(2)}) copy-start(f32[256,1024]{1,0:T(8,128)} %get-tuple-element.7) | copy-start | bytes 3145732
  116.3 1.0 copy-start.1
where the time goes:
time: 120 us; the launch traced here: 118 us
  Pallas kernels  111 us (92%)
  local copies, waits for them, and re-layouts  6.15 us (5%)
    pallas_call x1, Pallas kernels, fused(): pl.pallas_call(functools.partial(kernel, n), out_shape=(jax.ShapeDtypeStr...  111 us
    unnamed x8, local copies, waits for them, and re-layouts  6.15 us

commit v1 on v0

v1 whole, which is shorter than its diff:
```python
import functools

import jax
import jax.numpy as jnp
from jax import lax
from jax.experimental import pallas as pl
from jax.experimental.pallas import tpu as pltpu
from jax.sharding import PartitionSpec as P

MESH = pl.DeviceIdType.MESH
F32 = jnp.float32
BF16 = jnp.bfloat16
EARLY = 2


def split3(a):
    hi = a.astype(BF16)
    rest = a - hi.astype(F32)
    mid = rest.astype(BF16)
    low = (rest - mid.astype(F32)).astype(BF16)
    return jnp.concatenate([hi, mid, low], axis=0)


def tdot(a, b):
    return lax.dot_general(a, b, (((0,), (0,)), ((), ())), preferred_element_type=F32)


def plan(nu, ns, early):
    steps = []
    for u in range(nu):
        lead = u < nu // 2
        own = 2.0 + 0.2 * u if lead else (3.05 + 0.05 * (u - nu // 2) if u < nu - 2 else 5.15 + 0.05 * (u + 2 - nu))
        steps.append((own, "own", u))
        if u < early:
            steps.append((early + 0.1 + 0.25 * u, "prep", u))
            arrived = early + 0.2 + 0.25 * u
        else:
            arrived = u + 1.0
        steps.append((arrived, "other", u))
        if u % 2:
            steps.append((max(own + 0.01, 3.05 + 0.67 * (u - 1)), "own_out", u))
            steps.append((max(arrived + 0.01, 3.7 + 0.66 * (u - 1)), "other_out", u))
        if (u + 1) % (2 * ns) == 0:
            last = u == nu - 1
            steps.append((arrived + (0.1 if last else 1.5), "attn", u // (2 * ns)))
    steps.append((4.2, "own_attn", 0))
    steps.append((4.25, "memory", 0))
    return [step[1:] for step in sorted(steps, key=lambda step: step[0])]


def kernel(
    n, early, attn_hbm, w_hbm, g_hbm, rwt, gate, wpos, out_attn, out_w, out_mem,
    g, attn, w, attn_p, za, zb, zp, zpx, acc, onehot, mask, grow, rows, rows_x, local, after,
    gpad, grecv, lrecv, asend, arecv, ysend, yrecv, kept, zsend, zrecv, mine,
    g_sem, attn_sem, w_sem, xa_s, xa_r, xb_s, xb_r, gt_s, gt_r, l_s, l_r, a_s, a_r, r_s, r_r, t_s, t_r,
    p_s, p_r, q_s, q_r, y_s, y_r, z_s, z_r,
):
    d = lax.axis_index("dp")
    t = lax.axis_index("tensor")
    c = lax.rem(d, 2)
    y = lax.rem(d // 2, 2)
    z = d // 4
    nz = n // 4
    seg, half = g.shape
    hd = attn.shape[1]
    slots = rwt.shape[0]
    bw = 2 * half // n
    lw = half // n
    zh = nz // 2
    sub = mask.shape[1]
    ns = bw // sub
    nu = 2 * zh * ns
    oh = 1 - t
    pd = d + 1 - 2 * c
    partner = (pd, t)
    xpeer = (d, oh)
    ypeer = (d + 2 - 4 * y, t)
    tile = 256

    def remote(src, dst, ss, rs, dev):
        return pltpu.make_async_remote_copy(
            src_ref=src, dst_ref=dst, send_sem=ss, recv_sem=rs, device_id=dev, device_id_type=MESH
        )

    def peer(o):
        return lax.rem(d + o, n)

    barrier = pltpu.get_barrier_semaphore()
    for o in range(1, n):
        pl.semaphore_signal(barrier, inc=1, device_id=(peer(o), t), device_id_type=MESH)
    pl.semaphore_signal(barrier, inc=1, device_id=xpeer, device_id_type=MESH)
    pl.semaphore_signal(barrier, inc=1, device_id=(pd, oh), device_id_type=MESH)

    gcopy = pltpu.make_async_copy(g_hbm, g, g_sem)
    gcopy.start()
    attncopy = pltpu.make_async_copy(attn_hbm, attn, attn_sem)
    attncopy.start()
    gpad[...] = jnp.zeros_like(gpad)
    gpad[:, :slots] = gate[...].T
    three = split3(rwt[...])
    place_of = lax.broadcasted_iota(jnp.int32, (seg, slots), 0)
    hit = jnp.where(place_of == wpos[...], 1.0, 0.0)
    onehot[...] = hit.astype(BF16)
    mask[...] = jnp.broadcast_to(jnp.sum(hit, axis=1, keepdims=True), mask.shape)
    pl.semaphore_wait(barrier, n + 1)

    def is_other(u):
        return u % 2 == 0

    def level(h, r):
        return r + h * (zh - 1 - 2 * r)

    def cols(h, u, par):
        yd = 1 - y if is_other(u) else y
        j = 2 * level(h, u // (2 * ns)) + yd
        piece = u % (2 * ns) // 2
        return pl.ds(pl.multiple_of((2 * j + par) * bw + piece * sub, sub), sub)

    def wide(h, r):
        return pl.multiple_of(4 * level(h, r) * bw, 4 * bw)

    xa, xb = [], []
    for u in range(nu):
        mine_at, part_at = cols(t, u, c), cols(t, u, 1 - c)
        src = g_hbm if u < early else za
        xa.append(remote(src.at[:, mine_at], zb.at[:, mine_at], xa_s.at[u], xa_r.at[u], xpeer))
        if u < early:
            xb.append(remote(src.at[:, part_at], zb.at[:, part_at], xb_s.at[u], xb_r.at[u], xpeer))
        else:
            xb.append(remote(src.at[:, part_at], zpx.at[u], xb_s.at[u], xb_r.at[u], (pd, oh)))
    for u in range(early):
        xb[u].start()
        xa[u].start()

    grecv[0] = gpad[...]
    gcopies = [remote(gpad, grecv.at[o], gt_s.at[o], gt_r.at[o], (peer(o), t)) for o in range(1, n)]
    for copy in gcopies:
        copy.start()
    wcopy = pltpu.make_async_copy(w_hbm, w, w_sem)
    wcopy.start()
    tcopy = remote(attn_hbm, attn_p, t_s, t_r, partner)
    tcopy.start()
    gcopy.wait()

    def local_step(i, _):
        at = pl.ds(pl.multiple_of(i * tile, tile), tile)
        r = jnp.dot(three, g[:, at], preferred_element_type=F32)
        local[:, at] = r[:slots] + r[slots : 2 * slots] + r[2 * slots :]
        return 0

    lax.fori_loop(0, half // tile, local_step, 0)

    def slab(o):
        return pl.ds(pl.multiple_of(peer(o) * lw, lw), lw)

    lcopies = [
        remote(local.at[:, slab(o)], lrecv.at[o], l_s.at[o], l_r.at[o], (peer(o), t)) for o in range(1, n)
    ]
    for copy in lcopies:
        copy.start()
    lrecv[0] = local[:, slab(0)]

    def row_step(i, _):
        at = pl.ds(pl.multiple_of(i * tile, tile), tile)
        grow[:, at] = tdot(onehot[...], g[:, at])
        return 0

    lax.fori_loop(0, half // tile, row_step, 0)
    for copy in gcopies + lcopies:
        copy.wait_recv()

    def acopy(o, target):
        return remote(asend.at[o], arecv.at[o], a_s.at[o], a_r.at[o], (target, t))

    def sweep(i, carry):
        s = n - 1 - i
        slot = lax.rem(d - s + n, n)
        target = lax.rem(s - d + n, n)
        asend[target] = carry
        gates = grecv[slot]
        fresh = lrecv[slot]
        for k in range(slots):
            fresh = fresh + gates[:, k : k + 1] * carry[k : k + 1, :]

        @pl.when(target != 0)
        def _():
            acopy(target, s).start()

        return fresh

    lax.fori_loop(0, n, sweep, jnp.zeros((slots, lw), F32))
    acopies = [acopy(o, peer(o)) for o in range(1, n)]
    for o in range(n):
        if o:
            acopies[o - 1].wait_recv()
        src = lax.rem(d - o + n, n)
        at = pl.ds(pl.multiple_of(src * lw, lw), lw)
        got = arecv[o] if o else asend[0]
        after[:, at] = got
        rows[:, at] = (grow[:, at] + got).astype(BF16)
    rows_at = pl.ds(wide(t, 0), 4 * bw)
    rcopy = remote(rows.at[:, rows_at], rows_x.at[:, rows_at], r_s, r_r, xpeer)
    rcopy.start()

    def fix(src, new_rows, dst, at):
        picked = jnp.dot(onehot[...], new_rows[:, at], preferred_element_type=F32)
        dst[:, at] = jnp.where(mask[...] > 0.5, picked, src[:, at].astype(F32)).astype(BF16)

    pcopies = [
        remote(za.at[:, cols(t, u, 1 - c)], zp.at[u], p_s.at[u], p_r.at[u], partner) for u in range(nu)
    ]
    qcopies = []
    for u in range(nu):
        if u < early:
            qcopies.append(remote(zb.at[:, cols(oh, u, 1 - c)], zpx.at[u], q_s.at[u], q_r.at[u], partner))
        else:
            qcopies.append(remote(zpx.at[u], zb.at[:, cols(oh, u, c)], q_s.at[u], q_r.at[u], partner))

    def fix_own(u):
        fix(g, rows, za, cols(t, u, 1 - c))
        fix(g, rows, za, cols(t, u, c))
        pcopies[u].start()
        if u >= early:

            @pl.when(c == 0)
            def _():
                xa[u].start()
                xb[u].start()

            @pl.when(c == 1)
            def _():
                xb[u].start()
                xa[u].start()

    for u in [*range(early, min(early + 2, nu)), *range(early), *range(early + 2, nu)]:
        fix_own(u)

    ycopies, ncopies = {}, []

    def slot_of(own, u):
        return (0 if own else nu // 2) + u // 2

    def grad_block(own, u):
        slot = slot_of(own, u)
        zr, zq, at = (za, zp, cols(t, u, c)) if own else (zb, zpx, cols(oh, u, c))

        def step(m, _):
            ht = pl.ds(pl.multiple_of(m * tile, tile), tile)
            r = tdot(zr[:, at], attn[:, ht]) + tdot(zq[u], attn_p[:, ht])
            if is_other(u):
                ysend[slot, :, ht] = r.astype(BF16)
            else:
                kept[slot, :, ht] = r
            return 0

        lax.fori_loop(0, hd // tile, step, 0)
        if is_other(u):
            copy = remote(ysend.at[slot], yrecv.at[slot], y_s.at[slot], y_r.at[slot], ypeer)
            copy.start()
            ycopies[slot] = copy

    def to_owner(own, u):
        slot = slot_of(own, u)
        piece = u % (2 * ns) // 2
        h = t if own else oh
        zd = zh * h + level(h, u // (2 * ns))
        ycopies[slot].wait_recv()
        at_home = zd == z

        @pl.when(at_home)
        def _():
            mine[piece] = kept[slot] + yrecv[slot].astype(F32)

        @pl.when(jnp.logical_not(at_home))
        def _():
            o = lax.rem(zd - z + nz, nz)
            zsend[slot] = (kept[slot] + yrecv[slot].astype(F32)).astype(BF16)
            remote(
                zsend.at[slot],
                zrecv.at[o, piece],
                z_s.at[slot],
                z_r.at[o, piece],
                (zd * 4 + 2 * y + c, t),
            ).start()

        ncopies.append((at_home, slot))

    def own_attn():
        wcopy.wait()

        def step(m, _):
            at = pl.ds(pl.multiple_of(m * tile, tile), tile)
            k = pl.ds(pl.multiple_of(t * half, half), half)
            acc[:, at] = jnp.dot(za[...], w[k, at], preferred_element_type=F32)
            return 0

        lax.fori_loop(0, hd // tile, step, 0)

    def other_attn(r):
        from_at = wide(oh, r)
        last = r == zh - 1
        for u in range(2 * ns * r, 2 * ns * (r + 1)):
            if u >= early:
                qcopies[u].wait_recv()

        def step(m, _):
            at = pl.ds(pl.multiple_of(m * tile, tile), tile)
            k = pl.ds(pl.multiple_of(oh * half + from_at, 4 * bw), 4 * bw)
            total = acc[:, at] + jnp.dot(
                zb[:, pl.ds(from_at, 4 * bw)], w[k, at], preferred_element_type=F32
            )
            if last:
                out_attn[:, at] = total.astype(BF16)
            else:
                acc[:, at] = total
            return 0

        lax.fori_loop(0, hd // tile, step, 0)

    def memory():
        gates = gpad[...]

        def step(i, _):
            at = pl.ds(pl.multiple_of(i * tile, tile), tile)
            fresh = local[:, at]
            carry = after[:, at]
            for k in range(slots):
                fresh = fresh + gates[:, k : k + 1] * carry[k : k + 1, :]
            out_mem[:, at] = fresh
            return 0

        lax.fori_loop(0, half // tile, step, 0)

    waited = set()

    def once(name, copy):
        if name not in waited:
            waited.add(name)
            copy.wait_recv()

    attncopy.wait()
    for kind, u in plan(nu, ns, early):
        if kind == "own":
            once("attn", tcopy)
            pcopies[u].wait_recv()
            grad_block(True, u)
        elif kind == "prep":
            once("rows", rcopy)
            xb[u].wait_recv()
            fix(zb, rows_x, zb, cols(oh, u, 1 - c))
            qcopies[u].start()
            xa[u].wait_recv()
            fix(zb, rows_x, zb, cols(oh, u, c))
        elif kind == "other":
            if u < early:
                qcopies[u].wait_recv()
            else:
                xa[u].wait_recv()
                xb[u].wait_recv()
                qcopies[u].start()
            grad_block(False, u)
        elif kind == "own_out":
            to_owner(True, u)
        elif kind == "other_out":
            to_owner(False, u)
        elif kind == "own_attn":
            own_attn()
        elif kind == "attn":
            other_attn(u)
        else:
            memory()

    for piece in range(ns):
        total = mine[piece]
        for o in range(1, nz):
            remote(
                zrecv.at[o, piece], zrecv.at[o, piece], z_s.at[0], z_r.at[o, piece], ypeer
            ).wait_recv()
            total = total + zrecv[o, piece].astype(F32)
        out_w[pl.ds(piece * sub, sub), :] = total

    sent = xa + xb + gcopies + lcopies + acopies + pcopies + qcopies + list(ycopies.values())
    for copy in sent + [tcopy, rcopy]:
        copy.wait_send()
    for at_home, slot in ncopies:

        @pl.when(jnp.logical_not(at_home))
        def _():
            remote(
                zsend.at[slot], zrecv.at[0, 0], z_s.at[slot], z_r.at[0, 0], ypeer
            ).wait_send()


def fused(n, attn_out, out_proj_t, grad_out, read_weights, memory_gate, write_pos):
    seg, half = grad_out.shape
    hd = attn_out.shape[1]
    slots = write_pos.shape[1]
    depth = out_proj_t.shape[0]
    bw, lw, nz = depth // n, half // n, n // 4
    sub = 128
    ns = bw // sub
    nu = nz * ns
    early = EARLY
    V = pltpu.VMEM
    D = pltpu.SemaphoreType.DMA
    vmem = pl.BlockSpec(memory_space=pltpu.VMEM)
    return pl.pallas_call(
        functools.partial(kernel, n, early),
        out_shape=(
            jax.ShapeDtypeStruct((seg, hd), BF16),
            jax.ShapeDtypeStruct((bw, hd), F32),
            jax.ShapeDtypeStruct((slots, half), F32),
        ),
        in_specs=[pl.BlockSpec(memory_space=pl.ANY)] * 3 + [vmem] * 3,
        out_specs=(vmem, vmem, vmem),
        scratch_shapes=[
            V((seg, half), BF16),
            V((seg, hd), BF16),
            V((depth, hd), BF16),
            V((seg, hd), BF16),
            V((seg, half), BF16),
            V((seg, half), BF16),
            V((nu, seg, sub), BF16),
            V((nu, seg, sub), BF16),
            V((seg, hd), F32),
            V((seg, slots), BF16),
            V((seg, sub), F32),
            V((slots, half), F32),
            V((slots, half), BF16),
            V((slots, half), BF16),
            V((slots, half), F32),
            V((slots, half), F32),
            V((slots, 128), F32),
            V((n, slots, 128), F32),
            V((n, slots, lw), F32),
            V((n, slots, lw), F32),
            V((n, slots, lw), F32),
            V((nu, sub, hd), BF16),
            V((nu, sub, hd), BF16),
            V((nu, sub, hd), F32),
            V((nu, sub, hd), BF16),
            V((nz, ns, sub, hd), BF16),
            V((ns, sub, hd), F32),
            D,
            D,
            D,
            D((nu,)),
            D((nu,)),
            D((nu,)),
            D((nu,)),
            D((n,)),
            D((n,)),
            D((n,)),
            D((n,)),
            D((n,)),
            D((n,)),
            D,
            D,
            D,
            D,
            D((nu,)),
            D((nu,)),
            D((nu,)),
            D((nu,)),
            D((nu,)),
            D((nu,)),
            D((nu,)),
            D((nz, ns)),
        ],
        compiler_params=pltpu.CompilerParams(
            collective_id=0, has_side_effects=True, vmem_limit_bytes=62 * 1024 * 1024
        ),
    )(attn_out, out_proj_t, grad_out, read_weights.T, memory_gate, write_pos)


def plain(attn_out, out_proj_t, grad_out, read_weights, memory_gate, write_pos):
    high = lax.Precision.HIGHEST
    seg_len = attn_out.shape[0]
    slots = write_pos.shape[1]
    gate_at_step = memory_gate.T
    dy_cols = grad_out.astype(jnp.float32)
    local = jnp.dot(read_weights.T, dy_cols, precision=high, preferred_element_type=jnp.float32)
    all_gates, all_terms = (
        lax.all_gather(gate_at_step, "dp", axis=0, tiled=True),
        lax.all_gather(local, "dp", axis=0, tiled=True),
    )
    count = lax.axis_size("dp")
    mine = lax.axis_index("dp")

    def sweep(step, carry):
        which = (count - 1 - step).astype(jnp.int32)
        gate = lax.dynamic_slice_in_dim(all_gates, which * slots, slots, 0)
        term = lax.dynamic_slice_in_dim(all_terms, which * slots, slots, 0)
        fresh = jnp.dot(gate, carry, precision=high, preferred_element_type=jnp.float32) + term
        return jnp.where(which > mine, fresh, carry)

    after = lax.fori_loop(0, count, sweep, jnp.zeros_like(local))
    grad_memory = (
        jnp.dot(gate_at_step, after, precision=high, preferred_element_type=jnp.float32) + local
    )
    places = jnp.arange(seg_len, dtype=jnp.int32)
    onehot = (places[:, None] == write_pos[0][None, :]).astype(jnp.float32)
    written = jnp.dot(onehot, after, precision=high, preferred_element_type=jnp.float32)
    grad_z = (dy_cols + written).astype(jnp.bfloat16)
    full_z = lax.all_gather(grad_z, "tensor", axis=1, tiled=True)
    grad_attn = jnp.dot(full_z, out_proj_t, preferred_element_type=jnp.float32).astype(jnp.bfloat16)
    term = lax.dot_general(
        full_z, attn_out, (((0,), (0,)), ((), ())), preferred_element_type=jnp.float32
    )
    grad_weight = lax.psum_scatter(term, "dp", scatter_dimension=0, tiled=True)
    return (grad_attn, grad_weight, grad_memory)


def solution(mesh):
    n = mesh.shape["dp"]
    parts = mesh.shape["tensor"]

    def body(attn_out, out_proj_t, grad_out, read_weights, memory_gate, write_pos):
        half, hd = grad_out.shape[1], attn_out.shape[1]
        fits = (
            parts == 2
            and n // 4 == 4
            and half % (n * 128) == 0
            and half % 256 == 0
            and hd % 256 == 0
            and out_proj_t.shape[0] <= 4096
        )
        args = (attn_out, out_proj_t, grad_out, read_weights, memory_gate, write_pos)
        return fused(n, *args) if fits else plain(*args)

    return jax.shard_map(
        body,
        mesh=mesh,
        in_specs=(
            P("dp", "tensor"),
            P(None, "tensor"),
            P("dp", "tensor"),
            P("dp", None),
            P("dp", None),
            P("dp", None),
        ),
        out_specs=(P("dp", "tensor"), P("dp", "tensor"), P("dp", "tensor")),
        check_vma=False,
    )
```

time: 120 us -> 95.1 us (0.79); the launches traced: 118 us -> 94.9 us
  Pallas kernels: 111 us -> 89.8 us
  local copies, waits for them, and re-layouts: 6.15 us -> 4.44 us
    pallas_call x1, Pallas kernels: 111 us -> 89.8 us  [fused(): pl.pallas_call(functools.partial(kernel, n, early), out_shape=(jax.ShapeD...]
    unnamed x8 -> x7, local copies, waits for them, and re-layouts: 6.15 us -> 4.44 us
where the time goes in v1:
time: 95.1 us; the launch traced here: 94.9 us
  Pallas kernels  89.8 us (94%)
  local copies, waits for them, and re-layouts  4.44 us (5%)
    pallas_call x1, Pallas kernels, fused(): pl.pallas_call(functools.partial(kernel, n, early), out_shape=(jax.ShapeD...  89.8 us
    unnamed x7, local copies, waits for them, and re-layouts  4.44 us

profile of v1, /device:TPU:17, one launch (start us, length us, event | category | flops | bytes accessed | tf_op | source)
XLA Modules:
  0.0 94.9 jit_solution(10230461613913436892)
XLA Ops:
  0.6 89.8 %shard_map.85 = (bf16[768,1024]{1,0:T(8,128)(2,1)}, f32[256,1024]{1,0:T(8,128)}, f32[16,2048]{1,0:T(8,128)}) custom-call(bf16[768,1024]{1,0:T(8,128)(2,1)} %attn_hbm.1, bf16[4096,1024]{1,0:T(8,128)(2,1)} %w_hbm.1, bf16[768,2048]{1,0:T(8,128)(2,1)} %g_hbm.1, f32[16,768]{1,0:T(8,128)} %bitcast.1, f32[16,16]{1,0:T(8,128)} %gate.1, s32[1,16]{1,0:T(1,128)} %wpos.1), custom_call_target="tpu_custom_call" | custom-call | tf_op jit(solution)/shard_map/pallas_call | solution.py:407
  90.5 0.0 copy-start
  90.5 2.8 %copy.12 = bf16[768,1024]{1,0:T(8,128)(2,1)} copy(bf16[768,1024]{1,0:T(8,128)(2,1)} %get-tuple-element.6) | data formatting | bytes 3145728
  93.2 0.0 copy-done
  93.2 0.0 copy-start.1
  93.2 1.0 %copy.13 = f32[256,1024]{1,0:T(8,128)} copy(f32[256,1024]{1,0:T(8,128)S(1)} %copy-done) | data formatting | bytes 2097152
  94.2 0.1 copy-done.1
  94.3 0.7 copy.14
Async XLA Ops:
  90.5 2.8 %copy-start = (f32[256,1024]{1,0:T(8,128)S(1)}, f32[256,1024]{1,0:T(8,128)}, u32[]{:S(2)}) copy-start(f32[256,1024]{1,0:T(8,128)} %get-tuple-element.7) | copy-start | bytes 3145732
  93.2 1.0 %copy-start.1 = (f32[16,2048]{1,0:T(8,128)S(1)}, f32[16,2048]{1,0:T(8,128)}, u32[]{:S(2)}) copy-start(f32[16,2048]{1,0:T(8,128)} %get-tuple-element.8) | copy-start | bytes 393220

commit v2 on v1

--- a/solution.py
+++ b/solution.py
@@ -38,8 +38,13 @@
             arrived = u + 1.0
         steps.append((arrived, "other", u))
         if u % 2:
-            steps.append((max(own + 0.01, 3.05 + 0.67 * (u - 1)), "own_out", u))
-            steps.append((max(arrived + 0.01, 3.7 + 0.66 * (u - 1)), "other_out", u))
+            sent = max(own + 0.01, 3.05 + 0.67 * (u - 1))
+            steps.append((sent, "own_out", u))
+            steps.append((sent + 0.9, "own_pass", u))
+            sent = max(arrived + 0.01, 3.7 + 0.66 * (u - 1))
+            if u < nu - 1:
+                steps.append((sent, "other_out", u))
+            steps.append((sent + 0.9, "other_pass", u))
         if (u + 1) % (2 * ns) == 0:
             last = u == nu - 1
             steps.append((arrived + (0.1 if last else 1.5), "attn", u // (2 * ns)))
@@ -49,11 +54,11 @@
 
 
 def kernel(
-    n, early, attn_hbm, w_hbm, g_hbm, rwt, gate, wpos, out_attn, out_w, out_mem,
-    g, attn, w, attn_p, za, zb, zp, zpx, acc, onehot, mask, grow, rows, rows_x, local, after,
-    gpad, grecv, lrecv, asend, arecv, ysend, yrecv, kept, zsend, zrecv, mine,
-    g_sem, attn_sem, w_sem, xa_s, xa_r, xb_s, xb_r, gt_s, gt_r, l_s, l_r, a_s, a_r, r_s, r_r, t_s, t_r,
-    p_s, p_r, q_s, q_r, y_s, y_r, z_s, z_r,
+    n, early, attn_hbm, w_hbm, g_hbm, rwt_hbm, gate_hbm, wpos_hbm, out_attn, out_w, out_mem,
+    rwt, gate, wpos, g, attn, w, attn_p, za, zb, zp, zpx, acc, onehot, mask, grow, rows, rows_x, local, after,
+    gpad, grecv, lrecv, asend, arecv, ysend, yrecv, kept, zsend, zpass, zrecv, mine,
+    small_sem, g_sem, attn_sem, w_sem, xa_s, xa_r, xb_s, xb_r, gt_s, gt_r, l_s, l_r, a_s, a_r, r_s, r_r, t_s, t_r,
+    p_s, p_r, q_s, q_r, y_s, y_r, z_s, v_r, z_r,
 ):
     d = lax.axis_index("dp")
     t = lax.axis_index("tensor")
@@ -91,10 +96,18 @@
     pl.semaphore_signal(barrier, inc=1, device_id=xpeer, device_id_type=MESH)
     pl.semaphore_signal(barrier, inc=1, device_id=(pd, oh), device_id_type=MESH)
 
+    smalls = [
+        pltpu.make_async_copy(src, dst, small_sem.at[i])
+        for i, (src, dst) in enumerate(((rwt_hbm, rwt), (gate_hbm, gate), (wpos_hbm, wpos)))
+    ]
+    for copy in smalls:
+        copy.start()
     gcopy = pltpu.make_async_copy(g_hbm, g, g_sem)
     gcopy.start()
     attncopy = pltpu.make_async_copy(attn_hbm, attn, attn_sem)
     attncopy.start()
+    for copy in smalls:
+        copy.wait()
     gpad[...] = jnp.zeros_like(gpad)
     gpad[:, :slots] = gate[...].T
     three = split3(rwt[...])
@@ -198,9 +211,12 @@
         got = arecv[o] if o else asend[0]
         after[:, at] = got
         rows[:, at] = (grow[:, at] + got).astype(BF16)
-    rows_at = pl.ds(wide(t, 0), 4 * bw)
-    rcopy = remote(rows.at[:, rows_at], rows_x.at[:, rows_at], r_s, r_r, xpeer)
-    rcopy.start()
+    rcopies = {}
+    for u in range(early):
+        for k, at in enumerate((cols(t, u, 1 - c), cols(t, u, c))):
+            copy = remote(rows.at[:, at], rows_x.at[:, at], r_s.at[2 * u + k], r_r.at[2 * u + k], xpeer)
+            copy.start()
+            rcopies[u, k] = copy
 
     def fix(src, new_rows, dst, at):
         picked = jnp.dot(onehot[...], new_rows[:, at], preferred_element_type=F32)
@@ -235,18 +251,21 @@
     for u in [*range(early, min(early + 2, nu)), *range(early), *range(early + 2, nu)]:
         fix_own(u)
 
-    ycopies, ncopies = {}, []
+    ycopies = {}
 
     def slot_of(own, u):
         return (0 if own else nu // 2) + u // 2
 
+    def product(own, u, ht):
+        zr, zq, at = (za, zp, cols(t, u, c)) if own else (zb, zpx, cols(oh, u, c))
+        return tdot(zr[:, at], attn[:, ht]) + tdot(zq[u], attn_p[:, ht])
+
     def grad_block(own, u):
         slot = slot_of(own, u)
-        zr, zq, at = (za, zp, cols(t, u, c)) if own else (zb, zpx, cols(oh, u, c))
 
         def step(m, _):
             ht = pl.ds(pl.multiple_of(m * tile, tile), tile)
-            r = tdot(zr[:, at], attn[:, ht]) + tdot(zq[u], attn_p[:, ht])
+            r = product(own, u, ht)
             if is_other(u):
                 ysend[slot, :, ht] = r.astype(BF16)
             else:
@@ -259,31 +278,78 @@
             copy.start()
             ycopies[slot] = copy
 
+    outer = (z == 0) | (z == nz - 1)
+    low = z < zh
+    inner_z = jnp.where(low, zh - 1, zh)
+
+    def place(own, u):
+        zd = zh * (t if own else oh) + level(t if own else oh, u // (2 * ns))
+        across = (zd < zh) != low
+        return slot_of(own, u), u % (2 * ns) // 2, zd, zd == z, across
+
+    def at_chip(zt):
+        return (zt * 4 + 2 * y + c, t)
+
+    def to_relay(slot, ht, k):
+        return remote(
+            zsend.at[slot, :, ht], zpass.at[slot, :, ht], z_s.at[slot, k], v_r.at[slot, k], at_chip(inner_z)
+        )
+
+    def to_home(slot, piece, zd, k, ht, kind):
+        return remote(
+            zsend.at[slot, :, ht], zrecv.at[kind, piece, :, ht], z_s.at[slot, k], z_r.at[kind, piece], at_chip(zd)
+        )
+
+    def first_stage(own, u, total, ht, k):
+        slot, piece, zd, at_home, across = place(own, u)
+
+        @pl.when(at_home)
+        def _():
+            mine[piece, :, ht] = total
+
+        @pl.when(across & jnp.logical_not(outer))
+        def _():
+            kept[slot, :, ht] = total
+
+        @pl.when(across & outer)
+        def _():
+            zsend[slot, :, ht] = total.astype(BF16)
+            to_relay(slot, ht, k).start()
+
+        @pl.when(jnp.logical_not(across | at_home))
+        def _():
+            zsend[slot, :, ht] = total.astype(BF16)
+            to_home(slot, piece, zd, k, ht, 1).start()
+
+    def second_stage(own, u, ht, k):
+        slot, piece, zd, _, across = place(own, u)
+
+        @pl.when(across & jnp.logical_not(outer))
+        def _():
+            to_relay(slot, ht, k).wait_recv()
+            zsend[slot, :, ht] = (kept[slot, :, ht] + zpass[slot, :, ht].astype(F32)).astype(BF16)
+            to_home(slot, piece, zd, k, ht, 0).start()
+
+    every = pl.ds(0, hd)
+
     def to_owner(own, u):
         slot = slot_of(own, u)
-        piece = u % (2 * ns) // 2
-        h = t if own else oh
-        zd = zh * h + level(h, u // (2 * ns))
         ycopies[slot].wait_recv()
-        at_home = zd == z
-
-        @pl.when(at_home)
-        def _():
-            mine[piece] = kept[slot] + yrecv[slot].astype(F32)
-
-        @pl.when(jnp.logical_not(at_home))
-        def _():
-            o = lax.rem(zd - z + nz, nz)
-            zsend[slot] = (kept[slot] + yrecv[slot].astype(F32)).astype(BF16)
-            remote(
-                zsend.at[slot],
-                zrecv.at[o, piece],
-                z_s.at[slot],
-                z_r.at[o, piece],
-                (zd * 4 + 2 * y + c, t),
-            ).start()
-
-        ncopies.append((at_home, slot))
+        first_stage(own, u, kept[slot] + yrecv[slot].astype(F32), every, 0)
+
+    def last_block(u):
+        slot = slot_of(False, u)
+        ycopies[slot].wait_recv()
+        for k in range(hd // tile):
+            ht = pl.ds(k * tile, tile)
+            first_stage(False, u, product(False, u, ht) + yrecv[slot, :, ht].astype(F32), ht, k)
+
+    def pass_on(own, u):
+        if not own and u == nu - 1:
+            for k in range(hd // tile):
+                second_stage(own, u, pl.ds(k * tile, tile), k)
+        else:
+            second_stage(own, u, every, 0)
 
     def own_attn():
         wcopy.wait()
@@ -345,10 +411,11 @@
             pcopies[u].wait_recv()
             grad_block(True, u)
         elif kind == "prep":
-            once("rows", rcopy)
+            rcopies[u, 0].wait_recv()
             xb[u].wait_recv()
             fix(zb, rows_x, zb, cols(oh, u, 1 - c))
             qcopies[u].start()
+            rcopies[u, 1].wait_recv()
             xa[u].wait_recv()
             fix(zb, rows_x, zb, cols(oh, u, c))
         elif kind == "other":
@@ -358,9 +425,14 @@
                 xa[u].wait_recv()
                 xb[u].wait_recv()
                 qcopies[u].start()
-            grad_block(False, u)
+            if u < nu - 1:
+                grad_block(False, u)
+            else:
+                last_block(u)
         elif kind == "own_out":
             to_owner(True, u)
+        elif kind in ("own_pass", "other_pass"):
+            pass_on(kind == "own_pass", u)
         elif kind == "other_out":
             to_owner(False, u)
         elif kind == "own_attn":
@@ -372,23 +444,62 @@
 
     for piece in range(ns):
         total = mine[piece]
-        for o in range(1, nz):
-            remote(
-                zrecv.at[o, piece], zrecv.at[o, piece], z_s.at[0], z_r.at[o, piece], ypeer
-            ).wait_recv()
-            total = total + zrecv[o, piece].astype(F32)
+        for kind in range(2):
+            to_home(0, piece, z, 0, every, kind).wait_recv()
+            total = total + zrecv[kind, piece].astype(F32)
         out_w[pl.ds(piece * sub, sub), :] = total
 
     sent = xa + xb + gcopies + lcopies + acopies + pcopies + qcopies + list(ycopies.values())
-    for copy in sent + [tcopy, rcopy]:
+    for copy in sent + [tcopy, *rcopies.values()]:
         copy.wait_send()
-    for at_home, slot in ncopies:
-
-        @pl.when(jnp.logical_not(at_home))
-        def _():
-            remote(
-                zsend.at[slot], zrecv.at[0, 0], z_s.at[slot], z_r.at[0, 0], ypeer
-            ).wait_send()
+    for own in (True, False):
+        for u in range(1, nu, 2):
+            slot, _, _, at_home, _ = place(own, u)
+            last = not own and u == nu - 1
+
+            @pl.when(jnp.logical_not(at_home))
+            def _(slot=slot, last=last):
+                for k in range(hd // tile if last else 1):
+                    to_relay(slot, pl.ds(k * tile, tile) if last else every, k).wait_send()
+
+
+def settle(srcs, dsts, held, in_sem, out_sem):
+    moves = []
+    for src, dst, buf in zip(srcs, dsts, held):
+        rows = min(128, src.shape[0])
+        for i in range(src.shape[0] // rows):
+            at = pl.ds(i * rows, rows)
+            k = len(moves)
+            moves.append(
+                (
+                    pltpu.make_async_copy(src.at[at], buf.at[at], in_sem.at[k]),
+                    pltpu.make_async_copy(buf.at[at], dst.at[at], out_sem.at[k]),
+                )
+            )
+    for fetch, _ in moves:
+        fetch.start()
+    for fetch, put in moves:
+        fetch.wait()
+        put.start()
+    for _, put in moves:
+        put.wait()
+
+
+def settle_kernel(a, b, m, out_a, out_b, out_m, va, vb, vm, in_sem, out_sem):
+    settle((a, b, m), (out_a, out_b, out_m), (va, vb, vm), in_sem, out_sem)
+
+
+def settled(outs):
+    shapes = [jax.ShapeDtypeStruct(o.shape, o.dtype) for o in outs]
+    count = sum(o.shape[0] // min(128, o.shape[0]) for o in outs)
+    return pl.pallas_call(
+        settle_kernel,
+        out_shape=tuple(shapes),
+        in_specs=[pl.BlockSpec(memory_space=pl.ANY)] * 3,
+        out_specs=tuple([pl.BlockSpec(memory_space=pl.ANY)] * 3),
+        scratch_shapes=[pltpu.VMEM(o.shape, o.dtype) for o in outs]
+        + [pltpu.SemaphoreType.DMA((count,)), pltpu.SemaphoreType.DMA((count,))],
+    )(*outs)
 
 
 def fused(n, attn_out, out_proj_t, grad_out, read_weights, memory_gate, write_pos):
@@ -404,16 +515,19 @@
     V = pltpu.VMEM
     D = pltpu.SemaphoreType.DMA
     vmem = pl.BlockSpec(memory_space=pltpu.VMEM)
-    return pl.pallas_call(
+    outs = pl.pallas_call(
         functools.partial(kernel, n, early),
         out_shape=(
             jax.ShapeDtypeStruct((seg, hd), BF16),
             jax.ShapeDtypeStruct((bw, hd), F32),
             jax.ShapeDtypeStruct((slots, half), F32),
         ),
-        in_specs=[pl.BlockSpec(memory_space=pl.ANY)] * 3 + [vmem] * 3,
+        in_specs=[pl.BlockSpec(memory_space=pl.ANY)] * 6,
         out_specs=(vmem, vmem, vmem),
         scratch_shapes=[
+            V((slots, seg), F32),
+            V((slots, slots), F32),
+            V((1, slots), jnp.int32),
             V((seg, half), BF16),
             V((seg, hd), BF16),
             V((depth, hd), BF16),
@@ -439,8 +553,10 @@
             V((nu, sub, hd), BF16),
             V((nu, sub, hd), F32),
             V((nu, sub, hd), BF16),
-            V((nz, ns, sub, hd), BF16),
+            V((nu, sub, hd), BF16),
+            V((2, ns, sub, hd), BF16),
             V((ns, sub, hd), F32),
+            D((3,)),
             D,
             D,
             D,
@@ -454,23 +570,25 @@
             D((n,)),
             D((n,)),
             D((n,)),
+            D((2 * early,)),
+            D((2 * early,)),
             D,
             D,
-            D,
-            D,
-            D((nu,)),
-            D((nu,)),
-            D((nu,)),
-            D((nu,)),
-            D((nu,)),
-            D((nu,)),
-            D((nu,)),
-            D((nz, ns)),
+            D((nu,)),
+            D((nu,)),
+            D((nu,)),
+            D((nu,)),
+            D((nu,)),
+            D((nu,)),
+            D((nu, hd // 256)),
+            D((nu, hd // 256)),
+            D((2, ns)),
         ],
         compiler_params=pltpu.CompilerParams(
             collective_id=0, has_side_effects=True, vmem_limit_bytes=62 * 1024 * 1024
         ),
     )(attn_out, out_proj_t, grad_out, read_weights.T, memory_gate, write_pos)
+    return settled(outs)
 
 
 def plain(attn_out, out_proj_t, grad_out, read_weights, memory_gate, write_pos):

time: 95.1 us -> 92.8 us (0.976)
  local copies, waits for them, and re-layouts: 4.44 us -> 0 us
  Pallas kernels: 89.8 us -> 92 us
    unnamed x7 -> x0, local copies, waits for them, and re-layouts: 4.44 us -> none
    pallas_call x0 -> x1, Pallas kernels: none -> 2.68 us  [settled(): pl.pallas_call(settle_kernel, out_shape=tuple(shapes), in_specs=[pl.Block...]
where the time goes in v2:
time: 92.8 us; the launch traced here: 92.7 us
  Pallas kernels  92 us (99%)
    pallas_call x1, Pallas kernels, fused(): pl.pallas_call(functools.partial(kernel, n, early), out_shape=(jax.ShapeD...  89.4 us
    pallas_call x1, Pallas kernels, settled(): pl.pallas_call(settle_kernel, out_shape=tuple(shapes), in_specs=[pl.Block...  2.68 us

profile of v2, /device:TPU:17, one launch (start us, length us, event | category | flops | bytes accessed | tf_op | source)
XLA Modules:
  0.0 92.7 jit_solution(7028840737182522730)
XLA Ops:
  0.6 89.4 %shard_map.85 = (bf16[768,1024]{1,0:T(8,128)(2,1)}, f32[256,1024]{1,0:T(8,128)}, f32[16,2048]{1,0:T(8,128)}) custom-call(bf16[768,1024]{1,0:T(8,128)(2,1)} %attn_hbm.1, bf16[4096,1024]{1,0:T(8,128)(2,1)} %w_hbm.1, bf16[768,2048]{1,0:T(8,128)(2,1)} %g_hbm.1, f32[16,768]{1,0:T(8,128)} %bitcast.1, f32[16,16]{1,0:T(8,128)} %gate_hbm.1, s32[1,16]{1,0:T(1,128)} %wpos_hbm.1), custom_call_target="tpu_custom_call" | custom-call | tf_op jit(solution)/shard_map/pallas_call | solution.py:518
  90.0 2.7 %shard_map.86 = (bf16[768,1024]{1,0:T(8,128)(2,1)}, f32[256,1024]{1,0:T(8,128)}, f32[16,2048]{1,0:T(8,128)}) custom-call(bf16[768,1024]{1,0:T(8,128)(2,1)} %get-tuple-element.6.a, f32[256,1024]{1,0:T(8,128)} %get-tuple-element.7.b, f32[16,2048]{1,0:T(8,128)} %get-tuple-element.8.m), custom_call_target="tpu_custom_call" | custom-call | tf_op jit(solution)/shard_map/pallas_call | solution.py:495

commit v3 on v2

--- a/solution.py
+++ b/solution.py
@@ -44,10 +44,13 @@
             sent = max(arrived + 0.01, 3.7 + 0.66 * (u - 1))
             if u < nu - 1:
                 steps.append((sent, "other_out", u))
-            steps.append((sent + 0.9, "other_pass", u))
-        if (u + 1) % (2 * ns) == 0:
-            last = u == nu - 1
-            steps.append((arrived + (0.1 if last else 1.5), "attn", u // (2 * ns)))
+            steps.append((sent + (0.9 if u < nu - 1 else 0.1), "other_pass", u))
+        if (u + 1) % (2 * ns) == 0 and u < nu - 1:
+            steps.append((arrived + 1.5, "attn", u // (2 * ns)))
+        if u == nu - 2:
+            steps.append((arrived + 0.2, "attn_part", range(nu - 2 * ns, nu - 1)))
+        if u == nu - 1:
+            steps.append((arrived + 1.0, "attn_part", range(u, nu)))
     steps.append((4.2, "own_attn", 0))
     steps.append((4.25, "memory", 0))
     return [step[1:] for step in sorted(steps, key=lambda step: step[0])]
@@ -106,15 +109,6 @@
     gcopy.start()
     attncopy = pltpu.make_async_copy(attn_hbm, attn, attn_sem)
     attncopy.start()
-    for copy in smalls:
-        copy.wait()
-    gpad[...] = jnp.zeros_like(gpad)
-    gpad[:, :slots] = gate[...].T
-    three = split3(rwt[...])
-    place_of = lax.broadcasted_iota(jnp.int32, (seg, slots), 0)
-    hit = jnp.where(place_of == wpos[...], 1.0, 0.0)
-    onehot[...] = hit.astype(BF16)
-    mask[...] = jnp.broadcast_to(jnp.sum(hit, axis=1, keepdims=True), mask.shape)
     pl.semaphore_wait(barrier, n + 1)
 
     def is_other(u):
@@ -145,6 +139,10 @@
         xb[u].start()
         xa[u].start()
 
+    for copy in smalls:
+        copy.wait()
+    gpad[...] = jnp.zeros_like(gpad)
+    gpad[:, :slots] = gate[...].T
     grecv[0] = gpad[...]
     gcopies = [remote(gpad, grecv.at[o], gt_s.at[o], gt_r.at[o], (peer(o), t)) for o in range(1, n)]
     for copy in gcopies:
@@ -153,6 +151,7 @@
     wcopy.start()
     tcopy = remote(attn_hbm, attn_p, t_s, t_r, partner)
     tcopy.start()
+    three = split3(rwt[...])
     gcopy.wait()
 
     def local_step(i, _):
@@ -172,6 +171,11 @@
     for copy in lcopies:
         copy.start()
     lrecv[0] = local[:, slab(0)]
+
+    place_of = lax.broadcasted_iota(jnp.int32, (seg, slots), 0)
+    hit = jnp.where(place_of == wpos[...], 1.0, 0.0)
+    onehot[...] = hit.astype(BF16)
+    mask[...] = jnp.broadcast_to(jnp.sum(hit, axis=1, keepdims=True), mask.shape)
 
     def row_step(i, _):
         at = pl.ds(pl.multiple_of(i * tile, tile), tile)
@@ -364,7 +368,6 @@
 
     def other_attn(r):
         from_at = wide(oh, r)
-        last = r == zh - 1
         for u in range(2 * ns * r, 2 * ns * (r + 1)):
             if u >= early:
                 qcopies[u].wait_recv()
@@ -375,7 +378,25 @@
             total = acc[:, at] + jnp.dot(
                 zb[:, pl.ds(from_at, 4 * bw)], w[k, at], preferred_element_type=F32
             )
-            if last:
+            acc[:, at] = total
+            return 0
+
+        lax.fori_loop(0, hd // tile, step, 0)
+
+    def part_attn(units):
+        for u in units:
+            if u >= early:
+                qcopies[u].wait_recv()
+        places = [cols(oh, u, par) for u in units for par in range(2)]
+
+        def step(m, _):
+            at = pl.ds(pl.multiple_of(m * tile, tile), tile)
+            lhs = jnp.concatenate([zb[:, k] for k in places], axis=1)
+            rhs = jnp.concatenate(
+                [w[pl.ds(pl.multiple_of(oh * half + k.start, sub), sub), at] for k in places], axis=0
+            )
+            total = acc[:, at] + jnp.dot(lhs, rhs, preferred_element_type=F32)
+            if nu - 1 in units:
                 out_attn[:, at] = total.astype(BF16)
             else:
                 acc[:, at] = total
@@ -439,6 +460,8 @@
             own_attn()
         elif kind == "attn":
             other_attn(u)
+        elif kind == "attn_part":
+            part_attn(u)
         else:
             memory()
 
@@ -463,43 +486,25 @@
                     to_relay(slot, pl.ds(k * tile, tile) if last else every, k).wait_send()
 
 
-def settle(srcs, dsts, held, in_sem, out_sem):
-    moves = []
-    for src, dst, buf in zip(srcs, dsts, held):
-        rows = min(128, src.shape[0])
-        for i in range(src.shape[0] // rows):
-            at = pl.ds(i * rows, rows)
-            k = len(moves)
-            moves.append(
-                (
-                    pltpu.make_async_copy(src.at[at], buf.at[at], in_sem.at[k]),
-                    pltpu.make_async_copy(buf.at[at], dst.at[at], out_sem.at[k]),
-                )
-            )
-    for fetch, _ in moves:
-        fetch.start()
-    for fetch, put in moves:
-        fetch.wait()
-        put.start()
-    for _, put in moves:
-        put.wait()
-
-
-def settle_kernel(a, b, m, out_a, out_b, out_m, va, vb, vm, in_sem, out_sem):
-    settle((a, b, m), (out_a, out_b, out_m), (va, vb, vm), in_sem, out_sem)
+def settle_kernel(a, b, m, out_a, out_b, out_m, sems):
+    copies = [
+        pltpu.make_async_copy(src, dst, sems.at[i])
+        for i, (src, dst) in enumerate(((a, out_a), (b, out_b), (m, out_m)))
+    ]
+    for copy in copies:
+        copy.start()
+    for copy in copies:
+        copy.wait()
 
 
 def settled(outs):
-    shapes = [jax.ShapeDtypeStruct(o.shape, o.dtype) for o in outs]
-    count = sum(o.shape[0] // min(128, o.shape[0]) for o in outs)
     return pl.pallas_call(
         settle_kernel,
-        out_shape=tuple(shapes),
-        in_specs=[pl.BlockSpec(memory_space=pl.ANY)] * 3,
+        out_shape=tuple(jax.ShapeDtypeStruct(o.shape, o.dtype) for o in outs),
+        in_specs=[pl.BlockSpec(memory_space=pltpu.VMEM)] * 3,
         out_specs=tuple([pl.BlockSpec(memory_space=pl.ANY)] * 3),
-        scratch_shapes=[pltpu.VMEM(o.shape, o.dtype) for o in outs]
-        + [pltpu.SemaphoreType.DMA((count,)), pltpu.SemaphoreType.DMA((count,))],
-    )(*outs)
+        scratch_shapes=[pltpu.SemaphoreType.DMA((3,))],
+    )(*[pltpu.with_memory_space_constraint(o, pltpu.VMEM) for o in outs])
 
 
 def fused(n, attn_out, out_proj_t, grad_out, read_weights, memory_gate, write_pos):
@@ -517,11 +522,7 @@
     vmem = pl.BlockSpec(memory_space=pltpu.VMEM)
     outs = pl.pallas_call(
         functools.partial(kernel, n, early),
-        out_shape=(
-            jax.ShapeDtypeStruct((seg, hd), BF16),
-            jax.ShapeDtypeStruct((bw, hd), F32),
-            jax.ShapeDtypeStruct((slots, half), F32),
-        ),
+        out_shape=(V((seg, hd), BF16), V((bw, hd), F32), V((slots, half), F32)),
         in_specs=[pl.BlockSpec(memory_space=pl.ANY)] * 6,
         out_specs=(vmem, vmem, vmem),
         scratch_shapes=[
@@ -585,7 +586,7 @@
             D((2, ns)),
         ],
         compiler_params=pltpu.CompilerParams(
-            collective_id=0, has_side_effects=True, vmem_limit_bytes=62 * 1024 * 1024
+            collective_id=0, has_side_effects=True, vmem_limit_bytes=52 * 1024 * 1024
         ),
     )(attn_out, out_proj_t, grad_out, read_weights.T, memory_gate, write_pos)
     return settled(outs)

time: 92.8 us -> 87.5 us (0.943)
  Pallas kernels: 92 us -> 86.7 us
    pallas_call x2, Pallas kernels: 92 us -> 86.7 us  [the longest x1 85.1 us: fused(): pl.pallas_call(functools.partial(kernel, n, early), out_shape=(V((seg, hd...]
where the time goes in v3:
time: 87.5 us; the launch traced here: 87.3 us
  Pallas kernels  86.7 us (99%)
    pallas_call x1, Pallas kernels, fused(): pl.pallas_call(functools.partial(kernel, n, early), out_shape=(V((seg, hd...  85.1 us

profile of v3, /device:TPU:17, one launch (start us, length us, event | category | flops | bytes accessed | tf_op | source)
XLA Modules:
  0.0 87.3 jit_solution(10304792467123382491)
XLA Ops:
  0.6 85.1 %shard_map.85 = (bf16[768,1024]{1,0:T(8,128)(2,1)S(1)}, f32[256,1024]{1,0:T(8,128)S(1)}, f32[16,2048]{1,0:T(8,128)S(1)}) custom-call(bf16[768,1024]{1,0:T(8,128)(2,1)} %attn_hbm.1, bf16[4096,1024]{1,0:T(8,128)(2,1)} %w_hbm.1, bf16[768,2048]{1,0:T(8,128)(2,1)} %g_hbm.1, f32[16,768]{1,0:T(8,128)} %bitcast.1, f32[16,16]{1,0:T(8,128)} %gate_hbm.1, s32[1,16]{1,0:T(1,128)} %wpos_hbm.1), custom_call_target="tpu_custom_call" | custom-call | tf_op jit(solution)/shard_map/pallas_call | solution.py:523
  85.8 1.5 %shard_map.86 = (bf16[768,1024]{1,0:T(8,128)(2,1)}, f32[256,1024]{1,0:T(8,128)}, f32[16,2048]{1,0:T(8,128)}) custom-call(bf16[768,1024]{1,0:T(8,128)(2,1)S(1)} %get-tuple-element.6.a, f32[256,1024]{1,0:T(8,128)S(1)} %get-tuple-element.7.b, f32[16,2048]{1,0:T(8,128)S(1)} %get-tuple-element.8.m), custom_call_target="tpu_custom_call" | custom-call | tf_op jit(solution)/shard_map/pallas_call | solution.py:501

commit v4 on v3

--- a/solution.py
+++ b/solution.py
@@ -40,17 +40,18 @@
         if u % 2:
             sent = max(own + 0.01, 3.05 + 0.67 * (u - 1))
             steps.append((sent, "own_out", u))
-            steps.append((sent + 0.9, "own_pass", u))
+            steps.append((sent + 1.3, "own_pass", u))
             sent = max(arrived + 0.01, 3.7 + 0.66 * (u - 1))
             if u < nu - 1:
                 steps.append((sent, "other_out", u))
-            steps.append((sent + (0.9 if u < nu - 1 else 0.1), "other_pass", u))
+            steps.append((sent + (1.2 if u < nu - 1 else 0.1), "other_pass", u))
         if (u + 1) % (2 * ns) == 0 and u < nu - 1:
             steps.append((arrived + 1.5, "attn", u // (2 * ns)))
         if u == nu - 2:
-            steps.append((arrived + 0.2, "attn_part", range(nu - 2 * ns, nu - 1)))
+            steps.append((arrived + 0.2, "attn_part1", range(nu - 2 * ns, nu - 1)))
         if u == nu - 1:
-            steps.append((arrived + 1.0, "attn_part", range(u, nu)))
+            steps.append((arrived + 1.0, "attn_part0", range(nu - 2 * ns, nu - 1)))
+            steps.append((arrived + 1.1, "attn_part", range(u, nu)))
     steps.append((4.2, "own_attn", 0))
     steps.append((4.25, "memory", 0))
     return [step[1:] for step in sorted(steps, key=lambda step: step[0])]
@@ -60,7 +61,7 @@
     n, early, attn_hbm, w_hbm, g_hbm, rwt_hbm, gate_hbm, wpos_hbm, out_attn, out_w, out_mem,
     rwt, gate, wpos, g, attn, w, attn_p, za, zb, zp, zpx, acc, onehot, mask, grow, rows, rows_x, local, after,
     gpad, grecv, lrecv, asend, arecv, ysend, yrecv, kept, zsend, zpass, zrecv, mine,
-    small_sem, g_sem, attn_sem, w_sem, xa_s, xa_r, xb_s, xb_r, gt_s, gt_r, l_s, l_r, a_s, a_r, r_s, r_r, t_s, t_r,
+    small_sem, g_sem, attn_sem, w_sem, x_s, x_r, gt_s, gt_r, l_s, l_r, a_s, a_r, r_s, r_r, t_s, t_r,
     p_s, p_r, q_s, q_r, y_s, y_r, z_s, v_r, z_r,
 ):
     d = lax.axis_index("dp")
@@ -90,6 +91,12 @@
             src_ref=src, dst_ref=dst, send_sem=ss, recv_sem=rs, device_id=dev, device_id_type=MESH
         )
 
+    def all_sent(ref, sem):
+        remote(ref, ref, sem, sem, xpeer).wait_send()
+
+    def all_here(ref, sem):
+        remote(ref, ref, sem, sem, xpeer).wait_recv()
+
     def peer(o):
         return lax.rem(d + o, n)
 
@@ -130,11 +137,11 @@
     for u in range(nu):
         mine_at, part_at = cols(t, u, c), cols(t, u, 1 - c)
         src = g_hbm if u < early else za
-        xa.append(remote(src.at[:, mine_at], zb.at[:, mine_at], xa_s.at[u], xa_r.at[u], xpeer))
+        xa.append(remote(src.at[:, mine_at], zb.at[:, mine_at], x_s.at[0], x_r.at[u], xpeer))
         if u < early:
-            xb.append(remote(src.at[:, part_at], zb.at[:, part_at], xb_s.at[u], xb_r.at[u], xpeer))
+            xb.append(remote(src.at[:, part_at], zb.at[:, part_at], x_s.at[1], x_r.at[u], xpeer))
         else:
-            xb.append(remote(src.at[:, part_at], zpx.at[u], xb_s.at[u], xb_r.at[u], (pd, oh)))
+            xb.append(remote(src.at[:, part_at], zpx.at[u], x_s.at[1], x_r.at[u], (pd, oh)))
     for u in range(early):
         xb[u].start()
         xa[u].start()
@@ -144,7 +151,7 @@
     gpad[...] = jnp.zeros_like(gpad)
     gpad[:, :slots] = gate[...].T
     grecv[0] = gpad[...]
-    gcopies = [remote(gpad, grecv.at[o], gt_s.at[o], gt_r.at[o], (peer(o), t)) for o in range(1, n)]
+    gcopies = [remote(gpad, grecv.at[o], gt_s, gt_r, (peer(o), t)) for o in range(1, n)]
     for copy in gcopies:
         copy.start()
     wcopy = pltpu.make_async_copy(w_hbm, w, w_sem)
@@ -166,7 +173,7 @@
         return pl.ds(pl.multiple_of(peer(o) * lw, lw), lw)
 
     lcopies = [
-        remote(local.at[:, slab(o)], lrecv.at[o], l_s.at[o], l_r.at[o], (peer(o), t)) for o in range(1, n)
+        remote(local.at[:, slab(o)], lrecv.at[o], l_s, l_r, (peer(o), t)) for o in range(1, n)
     ]
     for copy in lcopies:
         copy.start()
@@ -183,11 +190,12 @@
         return 0
 
     lax.fori_loop(0, half // tile, row_step, 0)
-    for copy in gcopies + lcopies:
-        copy.wait_recv()
+    others = pl.ds(1, n - 1)
+    all_here(grecv.at[others], gt_r)
+    all_here(lrecv.at[others], l_r)
 
     def acopy(o, target):
-        return remote(asend.at[o], arecv.at[o], a_s.at[o], a_r.at[o], (target, t))
+        return remote(asend.at[o], arecv.at[o], a_s, a_r, (target, t))
 
     def sweep(i, carry):
         s = n - 1 - i
@@ -206,56 +214,68 @@
         return fresh
 
     lax.fori_loop(0, n, sweep, jnp.zeros((slots, lw), F32))
-    acopies = [acopy(o, peer(o)) for o in range(1, n)]
+    all_here(arecv.at[others], a_r)
     for o in range(n):
-        if o:
-            acopies[o - 1].wait_recv()
         src = lax.rem(d - o + n, n)
         at = pl.ds(pl.multiple_of(src * lw, lw), lw)
         got = arecv[o] if o else asend[0]
         after[:, at] = got
         rows[:, at] = (grow[:, at] + got).astype(BF16)
-    rcopies = {}
     for u in range(early):
-        for k, at in enumerate((cols(t, u, 1 - c), cols(t, u, c))):
-            copy = remote(rows.at[:, at], rows_x.at[:, at], r_s.at[2 * u + k], r_r.at[2 * u + k], xpeer)
+        for at in (cols(t, u, 1 - c), cols(t, u, c)):
+            copy = remote(rows.at[:, at], rows_x.at[:, at], r_s, r_r, xpeer)
             copy.start()
-            rcopies[u, k] = copy
 
     def fix(src, new_rows, dst, at):
         picked = jnp.dot(onehot[...], new_rows[:, at], preferred_element_type=F32)
         dst[:, at] = jnp.where(mask[...] > 0.5, picked, src[:, at].astype(F32)).astype(BF16)
 
     pcopies = [
-        remote(za.at[:, cols(t, u, 1 - c)], zp.at[u], p_s.at[u], p_r.at[u], partner) for u in range(nu)
+        remote(za.at[:, cols(t, u, 1 - c)], zp.at[u], p_s, p_r.at[u // (nu - 2)], partner) for u in range(nu)
     ]
     qcopies = []
+    groups = [[u] for u in range(early)]
+    groups += [list(range(max(early, 2 * ns * r), 2 * ns * (r + 1))) for r in range(zh)]
+    groups[-1].pop()
+    groups.append([nu - 1])
+    group_of = {u: k for k, group in enumerate(groups) for u in group}
     for u in range(nu):
+        got = q_r.at[group_of[u]]
         if u < early:
-            qcopies.append(remote(zb.at[:, cols(oh, u, 1 - c)], zpx.at[u], q_s.at[u], q_r.at[u], partner))
+            qcopies.append(remote(zb.at[:, cols(oh, u, 1 - c)], zpx.at[u], q_s, got, partner))
         else:
-            qcopies.append(remote(zpx.at[u], zb.at[:, cols(oh, u, c)], q_s.at[u], q_r.at[u], partner))
+            qcopies.append(remote(zpx.at[u], zb.at[:, cols(oh, u, c)], q_s, got, partner))
+
+    def blocks(count):
+        return zpx.at[pl.ds(0, count)]
+
+    def q_here(u):
+        all_here(blocks(len(groups[group_of[u]])), q_r.at[group_of[u]])
 
     def fix_own(u):
         fix(g, rows, za, cols(t, u, 1 - c))
         fix(g, rows, za, cols(t, u, c))
         pcopies[u].start()
-        if u >= early:
+        pair = [] if u < early or u == nu - 2 else [u] if u < nu - 2 else [nu - 2, nu - 1]
+        if pair:
 
             @pl.when(c == 0)
             def _():
-                xa[u].start()
-                xb[u].start()
+                for v in pair:
+                    xa[v].start()
+                for v in pair:
+                    xb[v].start()
 
             @pl.when(c == 1)
             def _():
-                xb[u].start()
-                xa[u].start()
+                for v in pair:
+                    xb[v].start()
+                for v in pair:
+                    xa[v].start()
 
     for u in [*range(early, min(early + 2, nu)), *range(early), *range(early + 2, nu)]:
         fix_own(u)
 
-    ycopies = {}
 
     def slot_of(own, u):
         return (0 if own else nu // 2) + u // 2
@@ -278,9 +298,19 @@
 
         lax.fori_loop(0, hd // tile, step, 0)
         if is_other(u):
-            copy = remote(ysend.at[slot], yrecv.at[slot], y_s.at[slot], y_r.at[slot], ypeer)
-            copy.start()
-            ycopies[slot] = copy
+            ycopy(slot, every, slot).start()
+
+    every = pl.ds(0, hd)
+
+    def ycopy(slot, ht, k):
+        return remote(ysend.at[slot, :, ht], yrecv.at[slot, :, ht], y_s, y_r.at[k], ypeer)
+
+    def last_sent_block(u):
+        slot = slot_of(False, u)
+        for k in range(hd // tile):
+            ht = pl.ds(k * tile, tile)
+            ysend[slot, :, ht] = product(False, u, ht).astype(BF16)
+            ycopy(slot, ht, slot + k).start()
 
     outer = (z == 0) | (z == nz - 1)
     low = z < zh
@@ -296,12 +326,12 @@
 
     def to_relay(slot, ht, k):
         return remote(
-            zsend.at[slot, :, ht], zpass.at[slot, :, ht], z_s.at[slot, k], v_r.at[slot, k], at_chip(inner_z)
+            zsend.at[slot, :, ht], zpass.at[slot, :, ht], z_s, v_r.at[slot + k], at_chip(inner_z)
         )
 
-    def to_home(slot, piece, zd, k, ht, kind):
+    def to_home(slot, piece, zd, ht, kind):
         return remote(
-            zsend.at[slot, :, ht], zrecv.at[kind, piece, :, ht], z_s.at[slot, k], z_r.at[kind, piece], at_chip(zd)
+            zsend.at[slot, :, ht], zrecv.at[kind, piece, :, ht], z_s, z_r.at[kind, piece], at_chip(zd)
         )
 
     def first_stage(own, u, total, ht, k):
@@ -323,7 +353,7 @@
         @pl.when(jnp.logical_not(across | at_home))
         def _():
             zsend[slot, :, ht] = total.astype(BF16)
-            to_home(slot, piece, zd, k, ht, 1).start()
+            to_home(slot, piece, zd, ht, 1).start()
 
     def second_stage(own, u, ht, k):
         slot, piece, zd, _, across = place(own, u)
@@ -332,21 +362,20 @@
         def _():
             to_relay(slot, ht, k).wait_recv()
             zsend[slot, :, ht] = (kept[slot, :, ht] + zpass[slot, :, ht].astype(F32)).astype(BF16)
-            to_home(slot, piece, zd, k, ht, 0).start()
-
-    every = pl.ds(0, hd)
+            to_home(slot, piece, zd, ht, 0).start()
 
     def to_owner(own, u):
         slot = slot_of(own, u)
-        ycopies[slot].wait_recv()
+        ycopy(slot, every, slot).wait_recv()
         first_stage(own, u, kept[slot] + yrecv[slot].astype(F32), every, 0)
 
     def last_block(u):
         slot = slot_of(False, u)
-        ycopies[slot].wait_recv()
         for k in range(hd // tile):
             ht = pl.ds(k * tile, tile)
-            first_stage(False, u, product(False, u, ht) + yrecv[slot, :, ht].astype(F32), ht, k)
+            total = product(False, u, ht)
+            ycopy(slot, ht, slot + k).wait_recv()
+            first_stage(False, u, total + yrecv[slot, :, ht].astype(F32), ht, k)
 
     def pass_on(own, u):
         if not own and u == nu - 1:
@@ -368,9 +397,8 @@
 
     def other_attn(r):
         from_at = wide(oh, r)
-        for u in range(2 * ns * r, 2 * ns * (r + 1)):
-            if u >= early:
-                qcopies[u].wait_recv()
+        if 2 * ns * (r + 1) > early:
+            q_here(2 * ns * (r + 1) - 1)
 
         def step(m, _):
             at = pl.ds(pl.multiple_of(m * tile, tile), tile)
@@ -384,9 +412,7 @@
         lax.fori_loop(0, hd // tile, step, 0)
 
     def part_attn(units):
-        for u in units:
-            if u >= early:
-                qcopies[u].wait_recv()
+        q_here(units[-1])
         places = [cols(oh, u, par) for u in units for par in range(2)]
 
         def step(m, _):
@@ -418,36 +444,32 @@
 
         lax.fori_loop(0, half // tile, step, 0)
 
-    waited = set()
-
-    def once(name, copy):
-        if name not in waited:
-            waited.add(name)
-            copy.wait_recv()
-
     attncopy.wait()
+    tcopy.wait_recv()
     for kind, u in plan(nu, ns, early):
         if kind == "own":
-            once("attn", tcopy)
-            pcopies[u].wait_recv()
+            if u == 0:
+                all_here(blocks(nu - 2), p_r.at[0])
+            if u == nu - 2:
+                all_here(blocks(2), p_r.at[1])
             grad_block(True, u)
         elif kind == "prep":
-            rcopies[u, 0].wait_recv()
-            xb[u].wait_recv()
+            if u == 0:
+                all_here(rows_x.at[:, pl.ds(0, 2 * early * sub)], r_r)
+            all_here(blocks(2), x_r.at[u])
             fix(zb, rows_x, zb, cols(oh, u, 1 - c))
             qcopies[u].start()
-            rcopies[u, 1].wait_recv()
-            xa[u].wait_recv()
             fix(zb, rows_x, zb, cols(oh, u, c))
         elif kind == "other":
             if u < early:
-                qcopies[u].wait_recv()
+                q_here(u)
             else:
-                xa[u].wait_recv()
-                xb[u].wait_recv()
+                all_here(blocks(2), x_r.at[u])
                 qcopies[u].start()
-            if u < nu - 1:
+            if u < nu - 2:
                 grad_block(False, u)
+            elif u < nu - 1:
+                last_sent_block(u)
             else:
                 last_block(u)
         elif kind == "own_out":
@@ -462,28 +484,33 @@
             other_attn(u)
         elif kind == "attn_part":
             part_attn(u)
+        elif kind in ("attn_part0", "attn_part1"):
+
+            @pl.when(c == int(kind[-1]))
+            def _(u=u):
+                part_attn(u)
+
         else:
             memory()
 
     for piece in range(ns):
         total = mine[piece]
         for kind in range(2):
-            to_home(0, piece, z, 0, every, kind).wait_recv()
+            to_home(0, piece, z, every, kind).wait_recv()
             total = total + zrecv[kind, piece].astype(F32)
         out_w[pl.ds(piece * sub, sub), :] = total
 
-    sent = xa + xb + gcopies + lcopies + acopies + pcopies + qcopies + list(ycopies.values())
-    for copy in sent + [tcopy, *rcopies.values()]:
-        copy.wait_send()
-    for own in (True, False):
-        for u in range(1, nu, 2):
-            slot, _, _, at_home, _ = place(own, u)
-            last = not own and u == nu - 1
-
-            @pl.when(jnp.logical_not(at_home))
-            def _(slot=slot, last=last):
-                for k in range(hd // tile if last else 1):
-                    to_relay(slot, pl.ds(k * tile, tile) if last else every, k).wait_send()
+    all_sent(zp, x_s.at[0])
+    all_sent(zp, x_s.at[1])
+    all_sent(zp, p_s)
+    all_sent(zp, q_s)
+    all_sent(grecv.at[others], gt_s)
+    all_sent(lrecv.at[others], l_s)
+    all_sent(arecv.at[others], a_s)
+    all_sent(rows.at[:, pl.ds(0, 2 * early * sub)], r_s)
+    all_sent(yrecv, y_s)
+    all_sent(zsend.at[pl.ds(0, nu - ns)], z_s)
+    tcopy.wait_send()
 
 
 def settle_kernel(a, b, m, out_a, out_b, out_m, sems):
@@ -516,6 +543,7 @@
     sub = 128
     ns = bw // sub
     nu = nz * ns
+    zh = nz // 2
     early = EARLY
     V = pltpu.VMEM
     D = pltpu.SemaphoreType.DMA
@@ -561,28 +589,26 @@
             D,
             D,
             D,
+            D((2,)),
             D((nu,)),
-            D((nu,)),
-            D((nu,)),
-            D((nu,)),
-            D((n,)),
-            D((n,)),
-            D((n,)),
-            D((n,)),
-            D((n,)),
-            D((n,)),
-            D((2 * early,)),
-            D((2 * early,)),
-            D,
-            D,
-            D((nu,)),
-            D((nu,)),
-            D((nu,)),
-            D((nu,)),
-            D((nu,)),
-            D((nu,)),
-            D((nu, hd // 256)),
-            D((nu, hd // 256)),
+            D,
+            D,
+            D,
+            D,
+            D,
+            D,
+            D,
+            D,
+            D,
+            D,
+            D,
+            D((2,)),
+            D,
+            D((early + zh + 1,)),
+            D,
+            D((nu - 1 + hd // 256,)),
+            D,
+            D((nu - 1 + hd // 256,)),
             D((2, ns)),
         ],
         compiler_params=pltpu.CompilerParams(

time: 87.5 us -> 84.6 us (0.967)
  Pallas kernels: 86.7 us -> 83.8 us
    pallas_call x1, Pallas kernels: 85.1 us -> 82.3 us  [fused(): pl.pallas_call(functools.partial(kernel, n, early), out_shape=(V((seg, hd...]
where the time goes in v4:
time: 84.6 us; the launch traced here: 84.5 us
  Pallas kernels  83.8 us (99%)
    pallas_call x1, Pallas kernels, fused(): pl.pallas_call(functools.partial(kernel, n, early), out_shape=(V((seg, hd...  82.3 us

profile of v4, /device:TPU:17, one launch (start us, length us, event | category | flops | bytes accessed | tf_op | source)
XLA Modules:
  0.0 84.5 jit_solution(13920333138470306877)
XLA Ops:
  0.6 82.3 %shard_map.85 = (bf16[768,1024]{1,0:T(8,128)(2,1)S(1)}, f32[256,1024]{1,0:T(8,128)S(1)}, f32[16,2048]{1,0:T(8,128)S(1)}) custom-call(bf16[768,1024]{1,0:T(8,128)(2,1)} %attn_hbm.1, bf16[4096,1024]{1,0:T(8,128)(2,1)} %w_hbm.1, bf16[768,2048]{1,0:T(8,128)(2,1)} %g_hbm.1, f32[16,768]{1,0:T(8,128)} %bitcast.1, f32[16,16]{1,0:T(8,128)} %gate_hbm.1, s32[1,16]{1,0:T(1,128)} %wpos_hbm.1), custom_call_target="tpu_custom_call" | custom-call | tf_op jit(solution)/shard_map/pallas_call | solution.py:551
  82.9 1.5 %shard_map.86 = (bf16[768,1024]{1,0:T(8,128)(2,1)}, f32[256,1024]{1,0:T(8,128)}, f32[16,2048]{1,0:T(8,128)}) custom-call(bf16[768,1024]{1,0:T(8,128)(2,1)S(1)} %get-tuple-element.6.a, f32[256,1024]{1,0:T(8,128)S(1)} %get-tuple-element.7.b, f32[16,2048]{1,0:T(8,128)S(1)} %get-tuple-element.8.m), custom_call_target="tpu_custom_call" | custom-call | tf_op jit(solution)/shard_map/pallas_call | solution.py:528

commit v5 on v4

--- a/solution.py
+++ b/solution.py
@@ -11,6 +11,7 @@
 F32 = jnp.float32
 BF16 = jnp.bfloat16
 EARLY = 2
+PARTS = 1
 
 
 def split3(a):
@@ -48,10 +49,11 @@
         if (u + 1) % (2 * ns) == 0 and u < nu - 1:
             steps.append((arrived + 1.5, "attn", u // (2 * ns)))
         if u == nu - 2:
-            steps.append((arrived + 0.2, "attn_part1", range(nu - 2 * ns, nu - 1)))
+            steps.append((arrived - 0.6, "attn_part", range(nu - 2 * ns, u)))
+            steps.append((arrived + 0.2, "attn_part1", [u]))
         if u == nu - 1:
-            steps.append((arrived + 1.0, "attn_part0", range(nu - 2 * ns, nu - 1)))
-            steps.append((arrived + 1.1, "attn_part", range(u, nu)))
+            steps.append((arrived + 1.0, "attn_part0", [u - 1]))
+            steps.append((arrived + 1.1, "attn_part", [u]))
     steps.append((4.2, "own_attn", 0))
     steps.append((4.25, "memory", 0))
     return [step[1:] for step in sorted(steps, key=lambda step: step[0])]
@@ -59,7 +61,7 @@
 
 def kernel(
     n, early, attn_hbm, w_hbm, g_hbm, rwt_hbm, gate_hbm, wpos_hbm, out_attn, out_w, out_mem,
-    rwt, gate, wpos, g, attn, w, attn_p, za, zb, zp, zpx, acc, onehot, mask, grow, rows, rows_x, local, after,
+    rwt, gate, wpos, g, attn, w, attn_p, za, zb, zp, zpx, acc, onehot, mask, grow, rows, early_rows, rows_x, local, after,
     gpad, grecv, lrecv, asend, arecv, ysend, yrecv, kept, zsend, zpass, zrecv, mine,
     small_sem, g_sem, attn_sem, w_sem, x_s, x_r, gt_s, gt_r, l_s, l_r, a_s, a_r, r_s, r_r, t_s, t_r,
     p_s, p_r, q_s, q_r, y_s, y_r, z_s, v_r, z_r,
@@ -115,7 +117,6 @@
     gcopy = pltpu.make_async_copy(g_hbm, g, g_sem)
     gcopy.start()
     attncopy = pltpu.make_async_copy(attn_hbm, attn, attn_sem)
-    attncopy.start()
     pl.semaphore_wait(barrier, n + 1)
 
     def is_other(u):
@@ -136,12 +137,13 @@
     xa, xb = [], []
     for u in range(nu):
         mine_at, part_at = cols(t, u, c), cols(t, u, 1 - c)
-        src = g_hbm if u < early else za
+        src = g if u < early else za
         xa.append(remote(src.at[:, mine_at], zb.at[:, mine_at], x_s.at[0], x_r.at[u], xpeer))
         if u < early:
             xb.append(remote(src.at[:, part_at], zb.at[:, part_at], x_s.at[1], x_r.at[u], xpeer))
         else:
             xb.append(remote(src.at[:, part_at], zpx.at[u], x_s.at[1], x_r.at[u], (pd, oh)))
+    gcopy.wait()
     for u in range(early):
         xb[u].start()
         xa[u].start()
@@ -155,11 +157,8 @@
     for copy in gcopies:
         copy.start()
     wcopy = pltpu.make_async_copy(w_hbm, w, w_sem)
-    wcopy.start()
     tcopy = remote(attn_hbm, attn_p, t_s, t_r, partner)
-    tcopy.start()
     three = split3(rwt[...])
-    gcopy.wait()
 
     def local_step(i, _):
         at = pl.ds(pl.multiple_of(i * tile, tile), tile)
@@ -178,6 +177,8 @@
     for copy in lcopies:
         copy.start()
     lrecv[0] = local[:, slab(0)]
+    attncopy.start()
+    tcopy.start()
 
     place_of = lax.broadcasted_iota(jnp.int32, (seg, slots), 0)
     hit = jnp.where(place_of == wpos[...], 1.0, 0.0)
@@ -214,6 +215,7 @@
         return fresh
 
     lax.fori_loop(0, n, sweep, jnp.zeros((slots, lw), F32))
+    wcopy.start()
     all_here(arecv.at[others], a_r)
     for o in range(n):
         src = lax.rem(d - o + n, n)
@@ -222,12 +224,13 @@
         after[:, at] = got
         rows[:, at] = (grow[:, at] + got).astype(BF16)
     for u in range(early):
-        for at in (cols(t, u, 1 - c), cols(t, u, c)):
-            copy = remote(rows.at[:, at], rows_x.at[:, at], r_s, r_r, xpeer)
-            copy.start()
+        for k, at in enumerate((cols(t, u, 1 - c), cols(t, u, c))):
+            early_rows[:, pl.ds((2 * u + k) * sub, sub)] = rows[:, at]
+    rcopy = remote(early_rows, rows_x, r_s, r_r, xpeer)
+    rcopy.start()
 
     def fix(src, new_rows, dst, at):
-        picked = jnp.dot(onehot[...], new_rows[:, at], preferred_element_type=F32)
+        picked = jnp.dot(onehot[...], new_rows, preferred_element_type=F32)
         dst[:, at] = jnp.where(mask[...] > 0.5, picked, src[:, at].astype(F32)).astype(BF16)
 
     pcopies = [
@@ -236,8 +239,8 @@
     qcopies = []
     groups = [[u] for u in range(early)]
     groups += [list(range(max(early, 2 * ns * r), 2 * ns * (r + 1))) for r in range(zh)]
-    groups[-1].pop()
-    groups.append([nu - 1])
+    groups[-1] = groups[-1][:-2]
+    groups += [[nu - 2], [nu - 1]]
     group_of = {u: k for k, group in enumerate(groups) for u in group}
     for u in range(nu):
         got = q_r.at[group_of[u]]
@@ -253,8 +256,8 @@
         all_here(blocks(len(groups[group_of[u]])), q_r.at[group_of[u]])
 
     def fix_own(u):
-        fix(g, rows, za, cols(t, u, 1 - c))
-        fix(g, rows, za, cols(t, u, c))
+        for at in (cols(t, u, 1 - c), cols(t, u, c)):
+            fix(g, rows[:, at], za, at)
         pcopies[u].start()
         pair = [] if u < early or u == nu - 2 else [u] if u < nu - 2 else [nu - 2, nu - 1]
         if pair:
@@ -455,11 +458,11 @@
             grad_block(True, u)
         elif kind == "prep":
             if u == 0:
-                all_here(rows_x.at[:, pl.ds(0, 2 * early * sub)], r_r)
+                rcopy.wait_recv()
             all_here(blocks(2), x_r.at[u])
-            fix(zb, rows_x, zb, cols(oh, u, 1 - c))
+            fix(zb, rows_x[:, pl.ds(2 * u * sub, sub)], zb, cols(oh, u, 1 - c))
             qcopies[u].start()
-            fix(zb, rows_x, zb, cols(oh, u, c))
+            fix(zb, rows_x[:, pl.ds((2 * u + 1) * sub, sub)], zb, cols(oh, u, c))
         elif kind == "other":
             if u < early:
                 q_here(u)
@@ -507,17 +510,19 @@
     all_sent(grecv.at[others], gt_s)
     all_sent(lrecv.at[others], l_s)
     all_sent(arecv.at[others], a_s)
-    all_sent(rows.at[:, pl.ds(0, 2 * early * sub)], r_s)
+    rcopy.wait_send()
     all_sent(yrecv, y_s)
     all_sent(zsend.at[pl.ds(0, nu - ns)], z_s)
     tcopy.wait_send()
 
 
 def settle_kernel(a, b, m, out_a, out_b, out_m, sems):
-    copies = [
-        pltpu.make_async_copy(src, dst, sems.at[i])
-        for i, (src, dst) in enumerate(((a, out_a), (b, out_b), (m, out_m)))
-    ]
+    copies = []
+    for src, dst, parts in ((a, out_a, PARTS), (b, out_b, PARTS), (m, out_m, 1)):
+        rows = src.shape[0] // parts
+        for i in range(parts):
+            at = pl.ds(i * rows, rows)
+            copies.append(pltpu.make_async_copy(src.at[at], dst.at[at], sems.at[len(copies)]))
     for copy in copies:
         copy.start()
     for copy in copies:
@@ -530,7 +535,7 @@
         out_shape=tuple(jax.ShapeDtypeStruct(o.shape, o.dtype) for o in outs),
         in_specs=[pl.BlockSpec(memory_space=pltpu.VMEM)] * 3,
         out_specs=tuple([pl.BlockSpec(memory_space=pl.ANY)] * 3),
-        scratch_shapes=[pltpu.SemaphoreType.DMA((3,))],
+        scratch_shapes=[pltpu.SemaphoreType.DMA((2 * PARTS + 1,))],
     )(*[pltpu.with_memory_space_constraint(o, pltpu.VMEM) for o in outs])
 
 
@@ -570,7 +575,8 @@
             V((seg, sub), F32),
             V((slots, half), F32),
             V((slots, half), BF16),
-            V((slots, half), BF16),
+            V((slots, 2 * early * sub), BF16),
+            V((slots, 2 * early * sub), BF16),
             V((slots, half), F32),
             V((slots, half), F32),
             V((slots, 128), F32),
@@ -604,7 +610,7 @@
             D,
             D((2,)),
             D,
-            D((early + zh + 1,)),
+            D((early + zh + 2,)),
             D,
             D((nu - 1 + hd // 256,)),
             D,

time: 84.6 us -> 84.4 us (level)
  no operation moved by 1% of the time
where the time goes in v5:
time: 84.4 us; the launch traced here: 84.3 us
  Pallas kernels  83.6 us (99%)
    pallas_call x1, Pallas kernels, fused(): pl.pallas_call(functools.partial(kernel, n, early), out_shape=(V((seg, hd...  82.1 us

profile of v5, /device:TPU:17, one launch (start us, length us, event | category | flops | bytes accessed | tf_op | source)
XLA Modules:
  0.0 84.3 jit_solution(1026999779260141942)
XLA Ops:
  0.6 82.1 %shard_map.85 = (bf16[768,1024]{1,0:T(8,128)(2,1)S(1)}, f32[256,1024]{1,0:T(8,128)S(1)}, f32[16,2048]{1,0:T(8,128)S(1)}) custom-call(bf16[768,1024]{1,0:T(8,128)(2,1)} %attn_hbm.1, bf16[4096,1024]{1,0:T(8,128)(2,1)} %w_hbm.1, bf16[768,2048]{1,0:T(8,128)(2,1)} %g_hbm.1, f32[16,768]{1,0:T(8,128)} %bitcast.1, f32[16,16]{1,0:T(8,128)} %gate_hbm.1, s32[1,16]{1,0:T(1,128)} %wpos_hbm.1), custom_call_target="tpu_custom_call" | custom-call | tf_op jit(solution)/shard_map/pallas_call | solution.py:556
  82.7 1.5 %shard_map.86 = (bf16[768,1024]{1,0:T(8,128)(2,1)}, f32[256,1024]{1,0:T(8,128)}, f32[16,2048]{1,0:T(8,128)}) custom-call(bf16[768,1024]{1,0:T(8,128)(2,1)S(1)} %get-tuple-element.6.a, f32[256,1024]{1,0:T(8,128)S(1)} %get-tuple-element.7.b, f32[16,2048]{1,0:T(8,128)S(1)} %get-tuple-element.8.m), custom_call_target="tpu_custom_call" | custom-call | tf_op jit(solution)/shard_map/pallas_call | solution.py:533

commit v6 on v5

--- a/solution.py
+++ b/solution.py
@@ -41,11 +41,11 @@
         if u % 2:
             sent = max(own + 0.01, 3.05 + 0.67 * (u - 1))
             steps.append((sent, "own_out", u))
-            steps.append((sent + 1.3, "own_pass", u))
+            steps.append((min(sent + 1.3, nu - 1.04) if u < nu - 1 else sent + 1.3, "own_pass", u))
             sent = max(arrived + 0.01, 3.7 + 0.66 * (u - 1))
             if u < nu - 1:
                 steps.append((sent, "other_out", u))
-            steps.append((sent + (1.2 if u < nu - 1 else 0.1), "other_pass", u))
+            steps.append((min(sent + 1.2, nu - 1.05) if u < nu - 1 else sent + 0.1, "other_pass", u))
         if (u + 1) % (2 * ns) == 0 and u < nu - 1:
             steps.append((arrived + 1.5, "attn", u // (2 * ns)))
         if u == nu - 2:
@@ -310,8 +310,8 @@
 
     def last_sent_block(u):
         slot = slot_of(False, u)
-        for k in range(hd // tile):
-            ht = pl.ds(k * tile, tile)
+        for k in range(2):
+            ht = pl.ds(k * (hd // 2), hd // 2)
             ysend[slot, :, ht] = product(False, u, ht).astype(BF16)
             ycopy(slot, ht, slot + k).start()
 
@@ -374,16 +374,18 @@
 
     def last_block(u):
         slot = slot_of(False, u)
-        for k in range(hd // tile):
-            ht = pl.ds(k * tile, tile)
+        for k in range(4):
+            ht = pl.ds(k * (hd // 4), hd // 4)
             total = product(False, u, ht)
-            ycopy(slot, ht, slot + k).wait_recv()
+            if k % 2 == 0:
+                at = pl.ds(k // 2 * (hd // 2), hd // 2)
+                ycopy(slot, at, slot + k // 2).wait_recv()
             first_stage(False, u, total + yrecv[slot, :, ht].astype(F32), ht, k)
 
     def pass_on(own, u):
         if not own and u == nu - 1:
-            for k in range(hd // tile):
-                second_stage(own, u, pl.ds(k * tile, tile), k)
+            for k in range(4):
+                second_stage(own, u, pl.ds(k * (hd // 4), hd // 4), k)
         else:
             second_stage(own, u, every, 0)
 

time: 84.4 us -> 84.1 us (level)
  no operation moved by 1% of the time
where the time goes in v6:
time: 84.1 us; the launch traced here: 83.9 us
  Pallas kernels  83.3 us (99%)
    pallas_call x1, Pallas kernels, fused(): pl.pallas_call(functools.partial(kernel, n, early), out_shape=(V((seg, hd...  81.7 us

profile of v6, /device:TPU:17, one launch (start us, length us, event | category | flops | bytes accessed | tf_op | source)
XLA Modules:
  0.0 83.9 jit_solution(13656790400437558710)
XLA Ops:
  0.6 81.7 %shard_map.85 = (bf16[768,1024]{1,0:T(8,128)(2,1)S(1)}, f32[256,1024]{1,0:T(8,128)S(1)}, f32[16,2048]{1,0:T(8,128)S(1)}) custom-call(bf16[768,1024]{1,0:T(8,128)(2,1)} %attn_hbm.1, bf16[4096,1024]{1,0:T(8,128)(2,1)} %w_hbm.1, bf16[768,2048]{1,0:T(8,128)(2,1)} %g_hbm.1, f32[16,768]{1,0:T(8,128)} %bitcast.1, f32[16,16]{1,0:T(8,128)} %gate_hbm.1, s32[1,16]{1,0:T(1,128)} %wpos_hbm.1), custom_call_target="tpu_custom_call" | custom-call | tf_op jit(solution)/shard_map/pallas_call | solution.py:558
  82.4 1.5 %shard_map.86 = (bf16[768,1024]{1,0:T(8,128)(2,1)}, f32[256,1024]{1,0:T(8,128)}, f32[16,2048]{1,0:T(8,128)}) custom-call(bf16[768,1024]{1,0:T(8,128)(2,1)S(1)} %get-tuple-element.6.a, f32[256,1024]{1,0:T(8,128)S(1)} %get-tuple-element.7.b, f32[16,2048]{1,0:T(8,128)S(1)} %get-tuple-element.8.m), custom_call_target="tpu_custom_call" | custom-call | tf_op jit(solution)/shard_map/pallas_call | solution.py:535
